TPU v7x, 128 devices: a whole 4x4x4 slice. The times are simulated.
128 devices in a mesh: ta: 2 (over core), gx: 64 (over z, y, x).
Axes of the slice: x: 4, y: 4, z: 4, core: 2. Of those that a mesh axis runs over, the one named last changes fastest.
Arguments:
- time_links: float32 [6, 2, 3, 3, 384, 4608], P('ta', None, None, None, 'gx'), may hold values from -1 to 1, as said below
Outputs:
- loop_planes: float32 [384, 2, 4608], P('gx', None, 'ta')
- correlator: float32 [384, 193], P('gx')
Inputs may be any that keep to these rules, and one draw needn't show every extreme that they name: At every site and time, the matrix time_links[t, 0] + i time_links[t, 1] is special unitary.
All inputs are finite; a program needn't handle non-finite values.
Results may differ from a plain program's by a relative error of at most 0.00029.
Values sent between devices are 32-bit elements; how exact they have to be, the bound alone decides.
No kernel may reach another device: no remote copies, remote signals or barrier semaphores. Data moves between devices by JAX's collectives and lax.ppermute only.
A program may use at most 64 MiB of HBM per device.

v0:
```python
import jax
import jax.numpy as jnp
from jax import lax
from jax.sharding import PartitionSpec as P


def prefix(value, axis, join, neutral):
    count, mine = (lax.axis_size(axis), lax.axis_index(axis))
    pieces = lax.all_gather(value, axis)
    subtotal = jnp.full_like(value, 0) + jnp.asarray(neutral, value.dtype)

    def step(position, subtotal):
        longer = join(subtotal, pieces[position])
        return jnp.where(position < mine, longer, subtotal)

    return lax.fori_loop(0, count - 1, step, subtotal)


def broadcast(value, axis, root):
    return lax.dynamic_index_in_dim(lax.all_gather(value, axis), root, 0, keepdims=False)


def sent_to_all(value, axis):
    copies = jnp.broadcast_to(value, (lax.axis_size(axis), *value.shape))
    return lax.all_to_all(copies, axis, split_axis=0, concat_axis=0, tiled=True)


def taken_together(value, axis):
    everything = sent_to_all(value, axis)
    return jnp.sum(everything, axis=0)


def complex_mul(left, right):
    terms_real = []
    terms_imag = []
    for middle in range(3):
        left_real = left[0][:, middle : middle + 1]
        left_imag = left[1][:, middle : middle + 1]
        right_real = right[0][middle : middle + 1]
        right_imag = right[1][middle : middle + 1]
        terms_real.append(left_real * right_real - left_imag * right_imag)
        terms_imag.append(left_real * right_imag + left_imag * right_real)
    return jnp.stack(
        [
            terms_real[0] + terms_real[1] + terms_real[2],
            terms_imag[0] + terms_imag[1] + terms_imag[2],
        ]
    )


def trace_third(matrix):
    return (matrix[:, 0, 0] + matrix[:, 1, 1] + matrix[:, 2, 2]) / 3.0


def correlation(own_rows, others):
    return lax.dot_general(
        own_rows,
        others,
        (((1,), (1,)), ((), ())),
        precision=lax.Precision.HIGHEST,
        preferred_element_type=jnp.float32,
    )


def by_separation(products, offset, longest, period):
    row_index = lax.broadcasted_iota(jnp.int32, products.shape, 0)
    column_index = lax.broadcasted_iota(jnp.int32, products.shape, 1)
    separation = offset + column_index - row_index
    separation = separation % period
    targets = jnp.arange(longest + 1, dtype=jnp.int32)
    selector = (separation[:, :, None] == targets).astype(jnp.float32)
    return jnp.sum(products[:, :, None] * selector, axis=1)


def per_device(time_links):
    local_product = time_links[0]
    for slice_index in range(1, time_links.shape[0]):
        local_product = complex_mul(local_product, time_links[slice_index])
    plane_sites = time_links.shape[-1]
    ta_count = lax.axis_size("ta")
    site_share = plane_sites // ta_count
    unit_matrix = jnp.broadcast_to(
        jnp.eye(3, dtype=jnp.float32)[:, :, None, None], local_product.shape[1:]
    )
    identity = jnp.stack([unit_matrix, jnp.zeros_like(unit_matrix)])
    earlier = prefix(local_product, "ta", complex_mul, identity)
    full_product = complex_mul(earlier, local_product)
    traces = broadcast(trace_third(full_product), "ta", ta_count - 1)
    own_share = lax.dynamic_slice_in_dim(traces, lax.axis_index("ta") * site_share, site_share, 2)
    loop_planes = jnp.transpose(own_share, (1, 0, 2))
    planes = loop_planes.shape[0]
    flat_width = loop_planes.shape[1] * loop_planes.shape[2]
    gx_count = lax.axis_size("gx")
    far_blocks = gx_count // 2
    longest = planes * far_blocks
    own_rows = loop_planes.reshape(planes, flat_width)
    shard_rows = lax.all_gather(loop_planes, "gx", axis=0, tiled=True)
    products = correlation(own_rows, shard_rows.reshape(shard_rows.shape[0], flat_width))
    totals_part = by_separation(
        products, -lax.axis_index("gx") * planes, longest, planes * gx_count
    )
    correlator = taken_together(totals_part, "ta") / plane_sites
    return (loop_planes, correlator)


def solution(mesh):
    in_specs = (P("ta", None, None, None, "gx", None),)
    out_specs = (P("gx", None, "ta"), P("gx", None))
    return jax.shard_map(
        per_device, mesh=mesh, in_specs=in_specs, out_specs=out_specs, check_vma=False
    )
```

profile of v0, /device:TPU:1, one launch (start us, length us, event | category | flops | bytes accessed | tf_op | source)
XLA Modules:
  0.0 150.9 jit_solution(14402750112683205446)
XLA Ops:
  7.2 0.0 all-gather.7.cloned.1.call-start
  7.2 5.7 %fusion.11 = (f32[1,1,1,3,6,4608]{5,1,4,3,2,0:T(1,128)S(1)}, f32[1,1,1,3,6,4608]{5,1,4,3,2,0:T(1,128)S(1)}, f32[1,1,1,3,6,4608]{5,1,4,3,2,0:T(1,128)S(1)}, f32[1...) fusion(f32[3,2,3,3,6,4608]{5,1,4,3,2,0:T(2,128)} %param.1), kind=kLoop, calls=%fused_computation.88 | loop fusion | bytes 7962624 | tf_op jit(solution)/shard_map/slice | solution.py:39
  12.9 3.9 %fusion.12 = (f32[1,1,3,3,6,4608]{5,1,4,3,2,0:T(1,128)S(1)}, f32[1,1,3,3,6,4608]{5,1,4,3,2,0:T(1,128)S(1)}) fusion(f32[3,2,3,3,6,4608]{5,1,4,3,2,0:T(2,128)} %param.1), kind=kLoop, calls=%fused_computation.89 | loop fusion | bytes 3981312 | tf_op jit(solution)/shard_map/slice | solution.py:37
  16.9 0.3 copy_bitcast_fusion
  17.2 0.1 slice_bitcast_fusion.30
  17.3 0.1 slice_bitcast_fusion.31
  17.4 0.1 copy_bitcast_fusion.8
  17.5 0.1 copy_bitcast_fusion.10
  17.7 0.1 copy_bitcast_fusion.12
  17.8 1.0 subtract_add_fusion.4
  18.7 0.1 slice_bitcast_fusion.24
  18.8 0.0 copy-start.1
  18.8 0.1 slice_bitcast_fusion.25
  18.9 0.0 copy-start.3
  18.9 0.0 copy-start.5
  19.0 0.0 copy-start.7
  19.0 0.1 copy_bitcast_fusion.2
  19.1 0.1 copy_bitcast_fusion.4
  19.2 0.1 copy_bitcast_fusion.6
  19.3 0.3 copy-done.1
  19.6 0.1 copy-done.3
  19.8 0.2 copy-done.5
  19.9 0.2 copy-done.7
  20.1 0.9 subtract_add_fusion.3
  21.0 1.8 %pad_maximum_fusion = f32[2,3,3,6,4608]{4,3,2,1,0:T(8,128)} fusion(f32[1,3,3,6,4608]{4,3,2,1,0:T(8,128)S(1)} %get-tuple-element.60, f32[1,3,3,6,4608]{4,3,2,1,0:T(8,128)S(1)} %get-tuple-element.59), kind=kLoop, calls=%fused_computation.2 | loop fusion | flops 497664 | bytes 3981312 | tf_op jit(solution)/shard_map/stack | solution.py:43
  22.8 0.0 all-gather.7.cloned.1.call-update
  22.8 0.2 all-gather.5.cloned.1.call-start
  23.0 1.0 copy.111
  24.1 1.0 copy.110
  25.1 1.0 copy.109
  26.1 0.0 copy-start.2
  26.1 0.0 copy-start.4
  26.1 0.0 copy-start.6
  26.1 1.0 copy.108
  27.0 1.0 copy.107
  28.0 0.2 copy.106
  28.3 0.0 copy-done.2
  28.3 0.0 copy-done.4
  28.3 0.0 copy-done.6
  28.3 0.0 copy-done.8
  28.3 3.7 %subtract_add_fusion.1 = (f32[3,3,6,4608]{3,1,2,0:T(4,128)S(1)}, f32[3,3,6,4608]{3,1,2,0:T(4,128)S(1)}) fusion(f32[3,6,4608]{2,0,1:T(4,128)} %copy.111, f32[3,6,4608]{2,1,0:T(8,128)S(1)} %get-tuple-element.81, f32[3,6,4608]{2,0,1:T(4,128)} %copy.110, f32[3,6,4608]{2,1,0:T(8,128)S(1)} %copy-done.6, f32[3,6,4608]{2,0,1:T(4,128)} %copy.109, ...), kind=kLoop, calls=%fused_computation.13 | loop fusion | flops 5474304 | bytes 5971968 | tf_op jit(solution)/shard_map/add | solution.py:45
  32.1 0.2 slice_bitcast_fusion.10
  32.3 0.2 slice_bitcast_fusion.12
  32.6 12.0 %all-gather.7.cloned.1.call-done = f32[4,3,3,6,4608]{4,3,2,1,0:T(8,128)} async-done(((f32[2,3,3,6,4608]{4,3,2,1,0:T(8,128)}), f32[4,3,3,6,4608]{4,3,2,1,0:T(8,128)}) %all-gather.7.cloned.1.call-update) | async-done | bytes 3981328 | tf_op jit(solution)/shard_map/all_gather | solution.py:9
  44.6 2.1 %broadcast_multiply_fusion.5 = (f32[3,6,4608]{2,1,0:T(8,128)S(1)}, f32[3,6,4608]{2,1,0:T(8,128)S(1)}, f32[3,6,4608]{2,1,0:T(8,128)S(1)}, f32[3,6,4608]{2,1,0:T(8...) fusion(f32[2,2,3,3,6,4608]{5,4,3,2,1,0:T(8,128)} %bitcast.120), kind=kLoop, calls=%fused_computation.71 | loop fusion | flops 497664 | bytes 3981312 | tf_op jit(solution)/shard_map/while/body/eval_jaxpr/mul | solution.py:41
  46.7 1.2 copy-done
  47.9 0.2 slice_bitcast_fusion.19
  48.1 0.9 subtract_add_fusion.2
  49.0 0.2 stack_broadcast_in_dim.2
  49.1 0.3 maximum_select_fusion
  49.5 0.2 slice_bitcast_fusion.1
  49.7 0.1 slice_bitcast_fusion.11
  49.8 0.1 slice_bitcast_fusion.13
  49.9 2.0 %subtract_add_fusion = (f32[1,3,3,6,4608]{4,2,3,1,0:T(4,128)S(1)}, f32[1,3,3,6,4608]{4,2,3,1,0:T(4,128)S(1)}) fusion(f32[3,6,4608]{2,0,1:T(4,128)S(1)} %get-tuple-element.75, f32[3,6,4608]{2,1,0:T(8,128)S(1)} %get-tuple-element.72, f32[3,6,4608]{2,0,1:T(4,128)S(1)} %get-tuple-element.69, f32[3,6,4608]{2,1,0:T(8,128)S(1)} %get-tuple-element.66, ...), kind=kLoop, calls=%fused_computation.11 | loop fusion | flops 5474304 | bytes 5971968 | tf_op jit(solution)/shard_map/add | solution.py:45
  51.9 0.7 fusion.6
  52.6 2.1 %all-gather.1 = f32[4,1,1,6,4608]{4,2,3,1,0:T(1,128)S(1)} all-gather(f32[2,1,1,6,4608]{4,2,3,1,0:T(1,128)S(1)} %fusion.6), channel_id=3, replica_groups=mesh['ta'=2,'gx'=64] {'ta'}, dimensions={0}, use_global_device_ids=true | all-gather | bytes 663552 | tf_op jit(solution)/shard_map/all_gather | solution.py:20
  54.7 0.1 copy.155
  54.8 0.7 copy.117
  55.5 0.0 all-gather.5.cloned.1.call-update
  55.6 74.8 %all-gather.5.cloned.1.call-done = f32[384,2,2304]{2,1,0:T(2,128)} async-done(((f32[6,2,2304]{2,1,0:T(2,128)}), f32[384,2,2304]{2,1,0:T(2,128)}) %all-gather.5.cloned.1.call-update) | async-done | bytes 7077904 | tf_op jit(solution)/shard_map/all_gather | solution.py:97
  130.4 8.5 %fusion.2 = f32[6,384]{1,0:T(8,128)S(1)} fusion(f32[384,2,2304]{2,1,0:T(2,128)} %all-gather.5.cloned.1.call-done, f32[2,6,2304]{2,0,1:T(2,128)S(1)} %bitcast.123), kind=kOutput, calls=%fused_computation.20 | convolution fusion | flops 127401984 | bytes 7197696 | tf_op jit(solution)/shard_map/dot_general | solution.py:56
  138.9 0.3 select_reduce_fusion
  139.3 4.2 %all_to_all.5 = f32[2,6,193]{2,1,0:T(8,128)S(1)} all-to-all(f32[2,6,193]{2,1,0:T(8,128)S(1)} %broadcast_in_dim.2), channel_id=1, replica_groups=mesh['ta'=2,'gx'=64] {'ta'}, dimensions={0} | all-to-all | bytes 18528 | tf_op jit(solution)/shard_map/all_to_all | solution.py:25
  143.5 0.6 broadcast_multiply_fusion.6
  (11 shorter events, 0.1 us)
Async XLA Ops:
  7.2 37.4 %all-gather.7.cloned.1.call-start = ((), (), s32[]{:S(2)}) async-start(), calls=%async_computation.2 | async-start | bytes 7962624 | tf_op jit(solution)/shard_map/all_gather | solution.py:9
  18.8 0.8 copy-start.1
  18.9 0.8 copy-start.3
  18.9 1.0 copy-start.5
  19.0 1.1 copy-start.7
  22.8 107.6 %all-gather.5.cloned.1.call-start = ((), (), s32[]{:S(2)}) async-start(), calls=%async_computation.1 | async-start | bytes 7188480 | tf_op jit(solution)/shard_map/all_gather | solution.py:97
  26.1 2.3 %copy-start.2 = (f32[3,6,4608]{2,1,0:T(8,128)S(1)}, f32[3,6,4608]{2,1,0:T(8,128)}, u32[]{:S(2)}) copy-start(f32[3,6,4608]{2,1,0:T(8,128)} %copy-done.1) | copy-start | bytes 995332
  26.1 2.3 %copy-start.4 = (f32[3,6,4608]{2,1,0:T(8,128)S(1)}, f32[3,6,4608]{2,1,0:T(8,128)}, u32[]{:S(2)}) copy-start(f32[3,6,4608]{2,1,0:T(8,128)} %copy-done.3) | copy-start | bytes 995332
  26.1 2.3 %copy-start.6 = (f32[3,6,4608]{2,1,0:T(8,128)S(1)}, f32[3,6,4608]{2,1,0:T(8,128)}, u32[]{:S(2)}) copy-start(f32[3,6,4608]{2,1,0:T(8,128)} %copy-done.5) | copy-start | bytes 995332
  27.0 1.3 copy-start.8
  44.6 3.3 %copy-start = (f32[4,3,3,6,4608]{4,3,2,1,0:T(8,128)S(1)}, f32[4,3,3,6,4608]{4,3,2,1,0:T(8,128)}, u32[]{:S(2)}) copy-start(f32[4,3,3,6,4608]{4,3,2,1,0:T(8,128)} %all-gather.7.cloned.1.call-done) | copy-start | bytes 11943940
Sparse Core Ops, SparseCore 0:
  22.9 21.6 all-gather.6
  55.7 74.7 all-gather.4
where the time goes:
time: 151 us
  waiting for transfers between devices  86.9 us (58%)
  local copies, waits for them, and re-layouts  20.2 us (13%)
  between operations  14.4 us (10%)
  other arithmetic  14.3 us (9%)
  matrix products  8.47 us (6%)
  blocking collectives  6.34 us (4%)
    all_gather x1, waiting for transfers between devices, per_device(): shard_rows = lax.all_gather(loop_planes, 'gx', axis=0, tiled=True)  74.8 us
    all_gather x1, waiting for transfers between devices, prefix(): pieces = lax.all_gather(value, axis)  12 us
    add x5, other arithmetic, complex_mul(): terms_real[0] + terms_real[1] + terms_real[2]  8.52 us
    dot_general x1, matrix products, correlation(): lax.dot_general(own_rows, others, (((1,), (1,)), ((), ())), precision=lax...  8.47 us
    mul x21, local copies, waits for them, and re-layouts, complex_mul(): terms_real.append(left_real * right_real - left_imag * right_imag)  7.1 us
    slice x1, local copies, waits for them, and re-layouts, complex_mul(): right_real = right[0][middle:middle + 1]  5.72 us
    all_to_all x1, blocking collectives, sent_to_all(): return lax.all_to_all(copies, axis, split_axis=0, concat_axis=0, tiled=True)  4.22 us
    slice x2, local copies, waits for them, and re-layouts, complex_mul(): left_real = left[0][:, middle:middle + 1]  3.92 us
  transfers between devices with their start and end apart: 2, of which 2 were waited for; matrix products, arithmetic and copies ran while one was open for 6% of the time, Pallas kernels for 0%

commit v1 on v0

v1 whole, which is shorter than its diff:
```python
import functools

import jax
import jax.numpy as jnp
from jax import lax
from jax.experimental import pallas as pl
from jax.experimental.layout import Layout, with_layout_constraint
from jax.experimental.pallas import tpu as pltpu
from jax.sharding import Mesh, PartitionSpec as P

F32 = jnp.float32
LANES = 128
WIDE = pltpu.CompilerParams(vmem_limit_bytes=58 * 2**20)
SMALL = pltpu.CompilerParams(vmem_limit_bytes=12 * 2**20)


def cross_conj(first, second):
    row = []
    for k in range(3):
        a, b = (k + 1) % 3, (k + 2) % 3
        (fa, ga), (fb, gb) = first[a], first[b]
        (sa, ta), (sb, tb) = second[a], second[b]
        real = (fa * sb - ga * tb) - (fb * sa - gb * ta)
        imag = (fb * ta + gb * sa) - (fa * tb + ga * sb)
        row.append((real, imag))
    return row


def rows_times(rows, matrix):
    out = []
    for row in rows:
        line = []
        for j in range(3):
            real = imag = None
            for m in range(3):
                (ar, ai), (br, bi) = row[m], matrix[m][j]
                re = ar * br - ai * bi
                im = ar * bi + ai * br
                real = re if real is None else real + re
                imag = im if imag is None else imag + im
            line.append((real, imag))
        out.append(line)
    return out


CHUNKS = ((0, 8), (8, 8), (16, 2))


def product_kernel(links_ref, send_ref, keep_ref):
    mine = lax.axis_index("ta")
    for half, out_ref in ((1 - mine, send_ref), (mine, keep_ref)):
        for start, count in CHUNKS:
            def load(t, i, j):
                return tuple(
                    links_ref[t, i, j, pl.ds(36 * half + 2 * start + c, count, stride=2), :]
                    for c in range(2)
                )

            rows = [[load(0, i, j) for j in range(3)] for i in range(2)]
            for t in (1, 2):
                matrix = [[load(t, i, j) for j in range(3)] for i in range(2)]
                matrix.append(cross_conj(matrix[0], matrix[1]))
                rows = rows_times(rows, matrix)
            for i in range(2):
                for j in range(3):
                    for c in range(2):
                        out_ref[6 * i + 2 * j + c, 0, pl.ds(start, count), :] = rows[i][j][c]


def trace_kernel(keep_ref, got_ref, planes_ref, msg_ref):
    msg_ref[...] = jnp.zeros_like(msg_ref)
    for p in range(6):
        for start, count in CHUNKS:
            def load(ref):
                rows = [
                    [
                        tuple(ref[6 * i + 2 * j + c, p, pl.ds(start, count), :] for c in range(2))
                        for j in range(3)
                    ]
                    for i in range(2)
                ]
                rows.append(cross_conj(rows[0], rows[1]))
                return rows

            own, other = load(keep_ref), load(got_ref)
            real = imag = None
            for i in range(3):
                for j in range(3):
                    (ar, ai), (br, bi) = own[i][j], other[j][i]
                    re = ar * br - ai * bi
                    im = ar * bi + ai * br
                    real = re if real is None else real + re
                    imag = im if imag is None else imag + im
            base = 36 * p + 2 * start
            planes_ref[pl.ds(base, count, stride=2), :] = real / 3.0
            planes_ref[pl.ds(base + 1, count, stride=2), :] = imag / 3.0
    lane = lax.broadcasted_iota(jnp.int32, (4, LANES), 1) // 32
    tails = []
    for p in range(6):
        for c in range(2):
            for slot in range(2):
                count = 9 if c == 0 else 7
                tiles = planes_ref[pl.ds(36 * p + 2 * slot + c, count, stride=4), :]
                msg_ref[pl.ds(16 * 9 * c + 6 * slot + p, count, stride=16), :] = tiles
        tails.append(planes_ref[pl.ds(36 * p + 28 + 1, 4, stride=2), :])
    for b in range(4):
        for row, members in ((12, (0, 1, 2, 3)), (13, (4, 5))):
            packed = jnp.zeros((4, LANES), F32)
            for place, p in enumerate(members):
                shift = (32 * (place - b)) % LANES
                moved = pltpu.roll(tails[p], shift, 1) if shift else tails[p]
                packed = jnp.where(lane == place, moved, packed)
            msg_ref[pl.ds(16 * b + row, 4, stride=64), :] = packed


def correlate_kernel(own_ref, next_ref, far_ref, out_ref, rows_ref, shift_ref):
    lane = lax.broadcasted_iota(jnp.int32, (16, LANES), 1)
    for z, ref in enumerate((own_ref, next_ref, far_ref)):
        for p in range(6):
            target = pl.ds(96 * z + p, 16, stride=6)
            for k in range(2):
                rows_ref[k, target, :] = ref[pl.ds(6 * k + p, 16, stride=16), :]
            tail = ref[pl.ds(12 + p // 4, 16, stride=16), :]
            shift = (-32 * (p % 4)) % LANES
            tail = pltpu.roll(tail, shift, 1) if shift else tail
            rows_ref[2, target, :] = jnp.where(lane < 32, tail, 0.0)
    rows = jnp.concatenate([rows_ref[k] for k in range(3)], axis=1)
    products = lax.dot_general(
        rows[:96],
        rows,
        (((1,), (1,)), ((), ())),
        precision=lax.Precision.HIGHEST,
        preferred_element_type=F32,
    )
    products = jnp.concatenate([products, jnp.zeros((96, 96), F32)], axis=1)
    row = lax.broadcasted_iota(jnp.int32, (96, 384), 0)
    for bit in (1, 2, 4):
        products = jnp.where((row & bit) != 0, pltpu.roll(products, 384 - bit, 1), products)
    for g in range(12):
        group = products[8 * g : 8 * g + 8]
        if g:
            group = pltpu.roll(group, 384 - 8 * g, 1)
        for k in range(2):
            shift_ref[k, pl.ds(8 * g, 8), :] = group[:, LANES * k : LANES * (k + 1)]
    out_ref[...] = jnp.zeros_like(out_ref)
    for p in range(6):
        for k in range(2):
            out_ref[pl.ds(8 * k + p, 16, stride=16), :] = shift_ref[k, pl.ds(p, 16, stride=6), :]


def vmem(count):
    return [pl.BlockSpec(memory_space=pltpu.VMEM)] * count


def per_device(time_links):
    links = with_layout_constraint(
        time_links.reshape(3, 2, 3, 3, 6, 36, LANES),
        Layout((0, 2, 3, 4, 5, 1, 6)),
    )
    links = jnp.transpose(links, (0, 2, 3, 4, 5, 1, 6)).reshape(3, 3, 3, 432, LANES)
    send, keep = pl.pallas_call(
        product_kernel,
        grid=(6,),
        in_specs=[pl.BlockSpec((3, 2, 3, 72, LANES), lambda x: (0, 0, 0, x, 0))],
        out_specs=[pl.BlockSpec((12, 1, 18, LANES), lambda x: (0, x, 0, 0))] * 2,
        out_shape=[jax.ShapeDtypeStruct((12, 6, 18, LANES), F32)] * 2,
        compiler_params=WIDE,
        name="product",
    )(links)
    got = lax.ppermute(send, "ta", [(0, 1), (1, 0)])
    planes, messages = pl.pallas_call(
        trace_kernel,
        in_specs=vmem(2),
        out_specs=vmem(2),
        out_shape=[
            jax.ShapeDtypeStruct((216, LANES), F32),
            jax.ShapeDtypeStruct((256, LANES), F32),
        ],
        compiler_params=SMALL,
        name="trace",
    )(keep, got)
    loop_planes = with_layout_constraint(
        planes.reshape(6, 18, 2, LANES).transpose(0, 2, 1, 3),
        Layout((0, 2, 1, 3)),
    ).reshape(6, 2, 2304)
    own = lax.all_to_all(
        messages.reshape(16, 16, LANES), ("y", "x"), split_axis=0, concat_axis=0, tiled=True
    ).reshape(256, LANES)
    following = lax.ppermute(own, "z", [((d + 1) % 4, d) for d in range(4)])
    opposite = lax.ppermute(own, "z", [((d + 2) % 4, d) for d in range(4)])
    partial = pl.pallas_call(
        correlate_kernel,
        in_specs=vmem(3),
        out_specs=pl.BlockSpec(memory_space=pltpu.VMEM),
        out_shape=jax.ShapeDtypeStruct((256, LANES), F32),
        scratch_shapes=[pltpu.VMEM((3, 288, LANES), F32), pltpu.VMEM((2, 96, LANES), F32)],
        compiler_params=SMALL,
        name="correlate",
    )(own, following, opposite)
    pieces = lax.all_to_all(
        partial.reshape(16, 16, LANES), ("y", "x"), split_axis=0, concat_axis=0, tiled=True
    )
    total = jnp.sum(pieces, axis=0)
    total = total + lax.ppermute(total, "ta", [(0, 1), (1, 0)])
    correlator = jnp.concatenate([total[0:6], total[8:14, :65]], axis=1) / 4608.0
    return loop_planes, correlator


def solution(mesh):
    grid = Mesh(mesh.devices.reshape(2, 4, 4, 4), ("ta", "z", "y", "x"))
    gx = ("z", "y", "x")
    return jax.shard_map(
        per_device,
        mesh=grid,
        in_specs=(P("ta", None, None, None, gx, None),),
        out_specs=(P(gx, None, "ta"), P(gx, None)),
        check_vma=False,
    )
```

time: 151 us -> 51.7 us (0.34)
  waiting for transfers between devices: 86.9 us -> 7.78 us
  local copies, waits for them, and re-layouts: 20.2 us -> 1.17 us
  blocking collectives: 6.34 us -> 24 us
  between operations: 14.4 us -> 0.65 us
  other arithmetic: 14.3 us -> 0.63 us
  starting transfers between devices: 0.26 us -> 9.26 us
  matrix products: 8.47 us -> 0 us
  Pallas kernels: 0 us -> 7.91 us
    all_gather x2 -> x0, waiting for transfers between devices: 86.9 us -> none  [the longest x1 74.8 us: per_device(): shard_rows = lax.all_gather(loop_planes, 'gx', axis=0, tiled=True)]
    all_to_all x1 -> x2, blocking collectives: 4.22 us -> 24 us  [the longest x1 13.5 us: per_device(): lax.all_to_all(messages.reshape(16, 16, LANES), ('y', 'x'), split_axis=0,...]
    slice x3 -> x2, local copies, waits for them, and re-layouts: 9.64 us -> 0.01 us  [the longest x1 0.01 us: per_device(): total[8:14, :65]]
    ppermute x0 -> x4, starting transfers between devices: none -> 9.26 us  [the longest x1 3.84 us: per_device(): total = total + lax.ppermute(total, 'ta', [(0, 1), (1, 0)])]
    add x6 -> x1, other arithmetic: 8.52 us -> 0.01 us  [per_device(): total = total + lax.ppermute(total, 'ta', [(0, 1), (1, 0)])]
    dot_general x1 -> x0, matrix products: 8.47 us -> none  [correlation(): lax.dot_general(own_rows, others, (((1,), (1,)), ((), ())), precision=lax...]
    pallas_call x0 -> x3, Pallas kernels: none -> 7.91 us  [the longest x1 5.82 us: per_device(): pl.pallas_call(product_kernel, grid=(6,), in_specs=[pl.BlockSpec((3, 2, 3...]
    ppermute x0 -> x4, waiting for transfers between devices: none -> 7.78 us  [the longest x1 2.77 us: per_device(): following = lax.ppermute(own, 'z', [((d + 1) % 4, d) for d in range(4)])]
  transfers between devices with their start and end apart: 2 -> 4, of which waited for: 2 -> 4; matrix products, arithmetic and copies ran while one was open for 6% -> 0% of each run, Pallas kernels for 0% -> 0%
where the time goes in v1:
time: 51.7 us; the launch traced here: 51.4 us
  blocking collectives  24 us (46%)
  starting transfers between devices  9.26 us (18%)
  Pallas kernels  7.91 us (15%)
  waiting for transfers between devices  7.78 us (15%)
  local copies, waits for them, and re-layouts  1.17 us (2%)
  between operations  0.65 us (1%)
  other arithmetic  0.63 us (1%)
    all_to_all x1, blocking collectives, per_device(): lax.all_to_all(messages.reshape(16, 16, LANES), ('y', 'x'), split_axis=0,...  13.5 us
    all_to_all x1, blocking collectives, per_device(): lax.all_to_all(partial.reshape(16, 16, LANES), ('y', 'x'), split_axis=0,...  10.5 us
    pallas_call x1, Pallas kernels, per_device(): pl.pallas_call(product_kernel, grid=(6,), in_specs=[pl.BlockSpec((3, 2, 3...  5.82 us
    ppermute x1, starting transfers between devices, per_device(): total = total + lax.ppermute(total, 'ta', [(0, 1), (1, 0)])  3.84 us
    ppermute x1, starting transfers between devices, per_device(): opposite = lax.ppermute(own, 'z', [((d + 2) % 4, d) for d in range(4)])  3.6 us
    ppermute x1, waiting for transfers between devices, per_device(): following = lax.ppermute(own, 'z', [((d + 1) % 4, d) for d in range(4)])  2.77 us
    ppermute x1, waiting for transfers between devices, per_device(): got = lax.ppermute(send, 'ta', [(0, 1), (1, 0)])  2.26 us
    ppermute x1, waiting for transfers between devices, per_device(): opposite = lax.ppermute(own, 'z', [((d + 2) % 4, d) for d in range(4)])  1.92 us
  transfers between devices with their start and end apart: 4, of which 4 were waited for; matrix products, arithmetic and copies ran while one was open for 0% of the time, Pallas kernels for 0%

profile of v1, /device:TPU:1, one launch (start us, length us, event | category | flops | bytes accessed | tf_op | source)
XLA Modules:
  0.0 51.4 jit_solution(2622044357082585324)
XLA Ops:
  0.6 5.8 %product.1 = (f32[12,6,18,128]{3,2,1,0:T(8,128)}, f32[12,6,18,128]{3,2,1,0:T(8,128)}) custom-call(f32[3,3,3,432,128]{4,3,2,1,0:T(8,128)} %bitcast.18), custom_call_target="tpu_custom_call" | custom-call | tf_op jit(solution)/shard_map/product/pallas_call | solution.py:161
  6.5 1.4 %collective-permute-start = (f32[12,6,18,128]{3,2,1,0:T(8,128)}, f32[12,6,18,128]{3,2,1,0:T(8,128)S(1)}, u32[]{:S(2)}, u32[]{:S(2)}) collective-permute-start(f32[12,6,18,128]{3,2,1,0:T(8,128)} %get-tuple-element.7), channel_id=1, source_target_pairs={{0,64},{64,0},{1,65},{65,1},{2,66},{66,2},{3,67},{67,3},{4,68},{68... | collective-permute-start | bytes 1990664 | tf_op jit(solution)/shard_map/ppermute | solution.py:170
  7.8 2.3 %collective-permute-done.got_ref = f32[12,6,18,128]{3,2,1,0:T(8,128)S(1)} collective-permute-done((f32[12,6,18,128]{3,2,1,0:T(8,128)}, f32[12,6,18,128]{3,2,1,0:T(8,128)S(1)}, u32[]{:S(2)}, u32[]{:S(2)}) %collective-permute-start) | collective-permute-done | bytes 663584 | tf_op jit(solution)/shard_map/ppermute | solution.py:170
  10.1 0.0 copy-start
  10.1 1.2 %copy-done = f32[12,6,18,128]{3,2,1,0:T(8,128)S(1)} copy-done((f32[12,6,18,128]{3,2,1,0:T(8,128)S(1)}, f32[12,6,18,128]{3,2,1,0:T(8,128)}, u32[]{:S(2)}) %copy-start) | copy-done | bytes 663576
  11.3 1.1 %trace.1 = (f32[216,128]{1,0:T(8,128)}, f32[256,128]{1,0:T(8,128)S(1)}) custom-call(f32[12,6,18,128]{3,2,1,0:T(8,128)S(1)} %copy-done, f32[12,6,18,128]{3,2,1,0:T(8,128)S(1)} %collective-permute-done.got_ref), custom_call_target="tpu_custom_call" | custom-call | tf_op jit(solution)/shard_map/trace/pallas_call | solution.py:171
  12.3 13.5 %all_to_all.10 = f32[16,16,128]{2,1,0:T(8,128)S(1)} all-to-all(f32[16,16,128]{2,1,0:T(8,128)S(1)} %bitcast.17), channel_id=1, replica_groups=mesh['ta'=2,'z'=4,'y'=4,'x'=4] {'y','x'}, dimensions={0} | all-to-all | bytes 262144 | tf_op jit(solution)/shard_map/all_to_all | solution.py:186
  25.8 3.6 %collective-permute-start.2 = (f32[256,128]{1,0:T(8,128)S(1)}, f32[256,128]{1,0:T(8,128)S(1)}, u32[]{:S(2)}, u32[]{:S(2)}) collective-permute-start(f32[256,128]{1,0:T(8,128)S(1)} %bitcast.13), channel_id=1, source_target_pairs={{32,0},{48,16},{0,32},{16,48},{33,1},{49,17},{1,33},{17,49},{34,2}... | collective-permute-start | bytes 393224 | tf_op jit(solution)/shard_map/ppermute | solution.py:190
  29.4 0.4 collective-permute-start.1
  29.9 1.9 %collective-permute-done.2.far_ref = f32[256,128]{1,0:T(8,128)S(1)} collective-permute-done((f32[256,128]{1,0:T(8,128)S(1)}, f32[256,128]{1,0:T(8,128)S(1)}, u32[]{:S(2)}, u32[]{:S(2)}) %collective-permute-start.2) | collective-permute-done | bytes 131104 | tf_op jit(solution)/shard_map/ppermute | solution.py:190
  31.8 2.8 %collective-permute-done.1.next_ref = f32[256,128]{1,0:T(8,128)S(1)} collective-permute-done((f32[256,128]{1,0:T(8,128)S(1)}, f32[256,128]{1,0:T(8,128)S(1)}, u32[]{:S(2)}, u32[]{:S(2)}) %collective-permute-start.1) | collective-permute-done | bytes 131104 | tf_op jit(solution)/shard_map/ppermute | solution.py:189
  34.6 1.0 %correlate.1 = f32[256,128]{1,0:T(8,128)S(1)} custom-call(f32[256,128]{1,0:T(8,128)S(1)} %bitcast.15, f32[256,128]{1,0:T(8,128)S(1)} %collective-permute-done.1.next_ref, f32[256,128]{1,0:T(8,128)S(1)} %collective-permute-done.2.far_ref), custom_call_target="tpu_custom_call" | custom-call | tf_op jit(solution)/shard_map/correlate/pallas_call | solution.py:191
  35.6 10.5 %all_to_all.11 = f32[16,16,128]{2,1,0:T(8,128)S(1)} all-to-all(f32[16,16,128]{2,1,0:T(8,128)S(1)} %bitcast.16), channel_id=1, replica_groups=mesh['ta'=2,'z'=4,'y'=4,'x'=4] {'y','x'}, dimensions={0} | all-to-all | bytes 262144 | tf_op jit(solution)/shard_map/all_to_all | solution.py:200
  46.1 3.8 %collective-permute-start.3 = (f32[16,128]{1,0:T(8,128)S(1)}, f32[16,128]{1,0:T(8,128)S(1)}, u32[]{:S(2)}, u32[]{:S(2)}) collective-permute-start(f32[16,128]{1,0:T(8,128)S(1)} %reduce_sum.9), channel_id=1, source_target_pairs={{0,64},{64,0},{1,65},{65,1},{2,66},{66,2},{3,67},{67,3},{4,68},{68... | collective-permute-start | bytes 24584 | tf_op jit(solution)/shard_map/ppermute | solution.py:204
  50.0 0.8 %collective-permute-done.3 = f32[16,128]{1,0:T(8,128)S(1)} collective-permute-done((f32[16,128]{1,0:T(8,128)S(1)}, f32[16,128]{1,0:T(8,128)S(1)}, u32[]{:S(2)}, u32[]{:S(2)}) %collective-permute-start.3) | collective-permute-done | bytes 8224 | tf_op jit(solution)/shard_map/ppermute | solution.py:204
  50.8 0.6 %maximum_multiply_fusion = f32[6,193]{1,0:T(8,128)} fusion(f32[6,65]{1,0:T(8,128)S(1)} %slice.9, f32[6,128]{1,0:T(8,128)S(1)} %slice.8), kind=kLoop, calls=%fused_computation | loop fusion | flops 2316 | bytes 9264 | tf_op jit(solution)/shard_map/div | solution.py:205
  (4 shorter events, 0.0 us)
Async XLA Ops:
  6.5 3.6 %collective-permute-start = (f32[12,6,18,128]{3,2,1,0:T(8,128)}, f32[12,6,18,128]{3,2,1,0:T(8,128)S(1)}, u32[]{:S(2)}, u32[]{:S(2)}) collective-permute-start(f32[12,6,18,128]{3,2,1,0:T(8,128)} %get-tuple-element.7), channel_id=1, source_target_pairs={{0,64},{64,0},{1,65},{65,1},{2,66},{66,2},{3,67},{67,3},{4,68},{68... | collective-permute-start | bytes 1990664 | tf_op jit(solution)/shard_map/ppermute | solution.py:170
  10.1 1.2 %copy-start = (f32[12,6,18,128]{3,2,1,0:T(8,128)S(1)}, f32[12,6,18,128]{3,2,1,0:T(8,128)}, u32[]{:S(2)}) copy-start(f32[12,6,18,128]{3,2,1,0:T(8,128)} %get-tuple-element.6.keep_ref) | copy-start | bytes 1990660
  25.8 6.0 %collective-permute-start.2 = (f32[256,128]{1,0:T(8,128)S(1)}, f32[256,128]{1,0:T(8,128)S(1)}, u32[]{:S(2)}, u32[]{:S(2)}) collective-permute-start(f32[256,128]{1,0:T(8,128)S(1)} %bitcast.13), channel_id=1, source_target_pairs={{32,0},{48,16},{0,32},{16,48},{33,1},{49,17},{1,33},{17,49},{34,2}... | collective-permute-start | bytes 393224 | tf_op jit(solution)/shard_map/ppermute | solution.py:190
  29.4 5.1 %collective-permute-start.1 = (f32[256,128]{1,0:T(8,128)S(1)}, f32[256,128]{1,0:T(8,128)S(1)}, u32[]{:S(2)}, u32[]{:S(2)}) collective-permute-start(f32[256,128]{1,0:T(8,128)S(1)} %bitcast.14), channel_id=1, source_target_pairs={{16,0},{32,16},{48,32},{0,48},{17,1},{33,17},{49,33},{1,49},{18,2}... | collective-permute-start | bytes 393224 | tf_op jit(solution)/shard_map/ppermute | solution.py:189
  46.1 4.7 %collective-permute-start.3 = (f32[16,128]{1,0:T(8,128)S(1)}, f32[16,128]{1,0:T(8,128)S(1)}, u32[]{:S(2)}, u32[]{:S(2)}) collective-permute-start(f32[16,128]{1,0:T(8,128)S(1)} %reduce_sum.9), channel_id=1, source_target_pairs={{0,64},{64,0},{1,65},{65,1},{2,66},{66,2},{3,67},{67,3},{4,68},{68... | collective-permute-start | bytes 24584 | tf_op jit(solution)/shard_map/ppermute | solution.py:204

commit v2 on v1

--- a/solution.py
+++ b/solution.py
@@ -10,7 +10,7 @@
 
 F32 = jnp.float32
 LANES = 128
-WIDE = pltpu.CompilerParams(vmem_limit_bytes=58 * 2**20)
+WIDE = pltpu.CompilerParams(vmem_limit_bytes=50 * 2**20)
 SMALL = pltpu.CompilerParams(vmem_limit_bytes=12 * 2**20)
 
 
@@ -46,13 +46,30 @@
 CHUNKS = ((0, 8), (8, 8), (16, 2))
 
 
-def product_kernel(links_ref, send_ref, keep_ref):
-    mine = lax.axis_index("ta")
-    for half, out_ref in ((1 - mine, send_ref), (mine, keep_ref)):
+def product_kernel(other, links_ref, out_ref, links, sems):
+    half = lax.axis_index("ta")
+    if other:
+        half = 1 - half
+    copies = []
+    for x in range(6):
+        source = pl.ds(pl.multiple_of(72 * x + 32 * half, 8), 40)
+        copies.append(
+            [
+                pltpu.make_async_copy(
+                    links_ref.at[t, pl.ds(0, 2), :, source, :], links.at[x, t], sems.at[x, t]
+                )
+                for t in range(3)
+            ]
+        )
+        for copy in copies[x]:
+            copy.start()
+    for x in range(6):
+        for copy in copies[x]:
+            copy.wait()
         for start, count in CHUNKS:
             def load(t, i, j):
                 return tuple(
-                    links_ref[t, i, j, pl.ds(36 * half + 2 * start + c, count, stride=2), :]
+                    links[x, t, i, j, pl.ds(4 * half + 2 * start + c, count, stride=2), :]
                     for c in range(2)
                 )
 
@@ -64,11 +81,30 @@
             for i in range(2):
                 for j in range(3):
                     for c in range(2):
-                        out_ref[6 * i + 2 * j + c, 0, pl.ds(start, count), :] = rows[i][j][c]
+                        out_ref[6 * i + 2 * j + c, x, pl.ds(start, count), :] = rows[i][j][c]
+
+
+def product(links, other):
+    return pl.pallas_call(
+        functools.partial(product_kernel, other),
+        in_specs=[pl.BlockSpec(memory_space=pltpu.HBM)],
+        out_specs=pl.BlockSpec(memory_space=pltpu.VMEM),
+        out_shape=jax.ShapeDtypeStruct((12, 6, 18, LANES), F32),
+        scratch_shapes=[
+            pltpu.VMEM((6, 3, 2, 3, 40, LANES), F32),
+            pltpu.SemaphoreType.DMA((6, 3)),
+        ],
+        compiler_params=WIDE,
+        cost_estimate=pl.CostEstimate(
+            flops=40_000_000, bytes_accessed=2_000_000, transcendentals=0
+        ),
+        name="product_sent" if other else "product_kept",
+    )(links)
 
 
 def trace_kernel(keep_ref, got_ref, planes_ref, msg_ref):
-    msg_ref[...] = jnp.zeros_like(msg_ref)
+    for d in range(16):
+        msg_ref[0, pl.ds(16 * d + 8, 8), :] = jnp.zeros((8, LANES), F32)
     for p in range(6):
         for start, count in CHUNKS:
             def load(ref):
@@ -101,7 +137,7 @@
             for slot in range(2):
                 count = 9 if c == 0 else 7
                 tiles = planes_ref[pl.ds(36 * p + 2 * slot + c, count, stride=4), :]
-                msg_ref[pl.ds(16 * 9 * c + 6 * slot + p, count, stride=16), :] = tiles
+                msg_ref[0, pl.ds(16 * 9 * c + 6 * slot + p, count, stride=16), :] = tiles
         tails.append(planes_ref[pl.ds(36 * p + 28 + 1, 4, stride=2), :])
     for b in range(4):
         for row, members in ((12, (0, 1, 2, 3)), (13, (4, 5))):
@@ -110,17 +146,21 @@
                 shift = (32 * (place - b)) % LANES
                 moved = pltpu.roll(tails[p], shift, 1) if shift else tails[p]
                 packed = jnp.where(lane == place, moved, packed)
-            msg_ref[pl.ds(16 * b + row, 4, stride=64), :] = packed
-
-
-def correlate_kernel(own_ref, next_ref, far_ref, out_ref, rows_ref, shift_ref):
+            msg_ref[0, pl.ds(16 * b + row, 4, stride=64), :] = packed
+    for z in range(1, 4):
+        msg_ref[z] = msg_ref[0]
+
+
+def correlate_kernel(got_ref, out_ref, rows_ref, shift_ref):
+    mine = lax.axis_index("z")
     lane = lax.broadcasted_iota(jnp.int32, (16, LANES), 1)
-    for z, ref in enumerate((own_ref, next_ref, far_ref)):
+    for z in range(3):
+        block = (mine + z) % 4
         for p in range(6):
             target = pl.ds(96 * z + p, 16, stride=6)
             for k in range(2):
-                rows_ref[k, target, :] = ref[pl.ds(6 * k + p, 16, stride=16), :]
-            tail = ref[pl.ds(12 + p // 4, 16, stride=16), :]
+                rows_ref[k, target, :] = got_ref[block, pl.ds(6 * k + p, 16, stride=16), :]
+            tail = got_ref[block, pl.ds(12 + p // 4, 16, stride=16), :]
             shift = (-32 * (p % 4)) % LANES
             tail = pltpu.roll(tail, shift, 1) if shift else tail
             rows_ref[2, target, :] = jnp.where(lane < 32, tail, 0.0)
@@ -158,23 +198,15 @@
         Layout((0, 2, 3, 4, 5, 1, 6)),
     )
     links = jnp.transpose(links, (0, 2, 3, 4, 5, 1, 6)).reshape(3, 3, 3, 432, LANES)
-    send, keep = pl.pallas_call(
-        product_kernel,
-        grid=(6,),
-        in_specs=[pl.BlockSpec((3, 2, 3, 72, LANES), lambda x: (0, 0, 0, x, 0))],
-        out_specs=[pl.BlockSpec((12, 1, 18, LANES), lambda x: (0, x, 0, 0))] * 2,
-        out_shape=[jax.ShapeDtypeStruct((12, 6, 18, LANES), F32)] * 2,
-        compiler_params=WIDE,
-        name="product",
-    )(links)
-    got = lax.ppermute(send, "ta", [(0, 1), (1, 0)])
+    got = lax.ppermute(product(links, True), "ta", [(0, 1), (1, 0)])
+    keep = product(links, False)
     planes, messages = pl.pallas_call(
         trace_kernel,
         in_specs=vmem(2),
         out_specs=vmem(2),
         out_shape=[
             jax.ShapeDtypeStruct((216, LANES), F32),
-            jax.ShapeDtypeStruct((256, LANES), F32),
+            jax.ShapeDtypeStruct((4, 256, LANES), F32),
         ],
         compiler_params=SMALL,
         name="trace",
@@ -183,20 +215,18 @@
         planes.reshape(6, 18, 2, LANES).transpose(0, 2, 1, 3),
         Layout((0, 2, 1, 3)),
     ).reshape(6, 2, 2304)
-    own = lax.all_to_all(
-        messages.reshape(16, 16, LANES), ("y", "x"), split_axis=0, concat_axis=0, tiled=True
-    ).reshape(256, LANES)
-    following = lax.ppermute(own, "z", [((d + 1) % 4, d) for d in range(4)])
-    opposite = lax.ppermute(own, "z", [((d + 2) % 4, d) for d in range(4)])
+    gathered = lax.all_to_all(
+        messages.reshape(64, 16, LANES), ("z", "y", "x"), split_axis=0, concat_axis=0, tiled=True
+    ).reshape(4, 256, LANES)
     partial = pl.pallas_call(
         correlate_kernel,
-        in_specs=vmem(3),
+        in_specs=vmem(1),
         out_specs=pl.BlockSpec(memory_space=pltpu.VMEM),
         out_shape=jax.ShapeDtypeStruct((256, LANES), F32),
         scratch_shapes=[pltpu.VMEM((3, 288, LANES), F32), pltpu.VMEM((2, 96, LANES), F32)],
         compiler_params=SMALL,
         name="correlate",
-    )(own, following, opposite)
+    )(gathered)
     pieces = lax.all_to_all(
         partial.reshape(16, 16, LANES), ("y", "x"), split_axis=0, concat_axis=0, tiled=True
     )

time: 51.7 us -> 46.4 us (0.90)
  blocking collectives: 24 us -> 33 us
  waiting for transfers between devices: 7.78 us -> 0.83 us
  starting transfers between devices: 9.26 us -> 4.7 us
  Pallas kernels: 7.91 us -> 6.29 us
  local copies, waits for them, and re-layouts: 1.17 us -> 0.01 us
    all_to_all x1, blocking collectives: 13.5 us -> 23.6 us  [per_device(): lax.all_to_all(messages.reshape(64, 16, LANES), ('z', 'y', 'x'), split_ax...]
    ppermute x3 -> x1, waiting for transfers between devices: 6.95 us -> 0.01 us  [per_device(): got = lax.ppermute(product(links, True), 'ta', [(0, 1), (1, 0)])]
    ppermute x3 -> x1, starting transfers between devices: 5.41 us -> 1.46 us  [per_device(): got = lax.ppermute(product(links, True), 'ta', [(0, 1), (1, 0)])]
    pallas_call x2 -> x3, Pallas kernels: 6.84 us -> 5.21 us  [the longest x2 4.19 us: product(): pl.pallas_call(functools.partial(product_kernel, other), in_specs=[pl.Blo...]
    unnamed x2 -> x0, local copies, waits for them, and re-layouts: 1.17 us -> none
    all_to_all x1, blocking collectives: 10.5 us -> 9.43 us  [per_device(): lax.all_to_all(partial.reshape(16, 16, LANES), ('y', 'x'), split_axis=0,...]
    ppermute x1, starting transfers between devices: 3.84 us -> 3.24 us  [per_device(): total = total + lax.ppermute(total, 'ta', [(0, 1), (1, 0)])]
  transfers between devices with their start and end apart: 4 -> 2, of which waited for: 4 -> 1; matrix products, arithmetic and copies ran while one was open for 0% -> 0% of each run, Pallas kernels for 0% -> 5%
where the time goes in v2:
time: 46.4 us; the launch traced here: 46.1 us
  blocking collectives  33 us (71%)
  Pallas kernels  6.29 us (14%)
  starting transfers between devices  4.7 us (10%)
  waiting for transfers between devices  0.83 us (2%)
  between operations  0.67 us (1%)
  other arithmetic  0.63 us (1%)
    all_to_all x1, blocking collectives, per_device(): lax.all_to_all(messages.reshape(64, 16, LANES), ('z', 'y', 'x'), split_ax...  23.6 us
    all_to_all x1, blocking collectives, per_device(): lax.all_to_all(partial.reshape(16, 16, LANES), ('y', 'x'), split_axis=0,...  9.43 us
    pallas_call x2, Pallas kernels, product(): pl.pallas_call(functools.partial(product_kernel, other), in_specs=[pl.Blo...  4.19 us
    ppermute x1, starting transfers between devices, per_device(): total = total + lax.ppermute(total, 'ta', [(0, 1), (1, 0)])  3.24 us
    ppermute x1, starting transfers between devices, per_device(): got = lax.ppermute(product(links, True), 'ta', [(0, 1), (1, 0)])  1.46 us
    pallas_call x1, Pallas kernels, per_device(): pl.pallas_call(trace_kernel, in_specs=vmem(2), out_specs=vmem(2), out_sha...  1.08 us
    pallas_call x1, Pallas kernels, per_device(): pl.pallas_call(correlate_kernel, in_specs=vmem(1), out_specs=pl.BlockSpec...  1.01 us
  transfers between devices with their start and end apart: 2, of which 1 were waited for; matrix products, arithmetic and copies ran while one was open for 0% of the time, Pallas kernels for 5%

profile of v2, /device:TPU:1, one launch (start us, length us, event | category | flops | bytes accessed | tf_op | source)
XLA Modules:
  0.0 46.1 jit_solution(7432659926299178027)
XLA Ops:
  0.6 2.1 %product_sent.1 = f32[12,6,18,128]{3,2,1,0:T(8,128)S(1)} custom-call(f32[3,3,3,432,128]{4,3,2,1,0:T(8,128)} %bitcast.16), custom_call_target="tpu_custom_call" | custom-call | flops 40000000 | bytes 2000000 | tf_op jit(solution)/shard_map/product_sent/pallas_call | solution.py:88
  2.7 1.5 %collective-permute-start = (f32[12,6,18,128]{3,2,1,0:T(8,128)S(1)}, f32[12,6,18,128]{3,2,1,0:T(8,128)S(1)}, u32[]{:S(2)}, u32[]{:S(2)}) collective-permute-start(f32[12,6,18,128]{3,2,1,0:T(8,128)S(1)} %product_sent.1), channel_id=1, source_target_pairs={{0,64},{64,0},{1,65},{65,1},{2,66},{66,2},{3,67},{67,3},{4,68},{68... | collective-permute-start | bytes 1990664 | tf_op jit(solution)/shard_map/ppermute | solution.py:201
  4.2 2.1 %product_kept.1.keep_ref = f32[12,6,18,128]{3,2,1,0:T(8,128)S(1)} custom-call(f32[3,3,3,432,128]{4,3,2,1,0:T(8,128)} %bitcast.17), custom_call_target="tpu_custom_call" | custom-call | flops 40000000 | bytes 2000000 | tf_op jit(solution)/shard_map/product_kept/pallas_call | solution.py:88
  6.3 0.0 collective-permute-done.got_ref
  6.3 1.1 %trace.1 = (f32[216,128]{1,0:T(8,128)}, f32[4,256,128]{2,1,0:T(8,128)S(1)}) custom-call(f32[12,6,18,128]{3,2,1,0:T(8,128)S(1)} %product_kept.1.keep_ref, f32[12,6,18,128]{3,2,1,0:T(8,128)S(1)} %collective-permute-done.got_ref), custom_call_target="tpu_custom_call" | custom-call | tf_op jit(solution)/shard_map/trace/pallas_call | solution.py:203
  7.4 23.6 %all_to_all.10 = f32[64,16,128]{2,1,0:T(8,128)S(1)} all-to-all(f32[64,16,128]{2,1,0:T(8,128)S(1)} %bitcast.15), channel_id=1, replica_groups=mesh['ta'=2,'z'=4,'y'=4,'x'=4] {'z','y','x'}, dimensions={0} | all-to-all | bytes 1048576 | tf_op jit(solution)/shard_map/all_to_all | solution.py:218
  31.0 1.0 %correlate.1 = f32[256,128]{1,0:T(8,128)S(1)} custom-call(f32[4,256,128]{2,1,0:T(8,128)S(1)} %bitcast.13), custom_call_target="tpu_custom_call" | custom-call | tf_op jit(solution)/shard_map/correlate/pallas_call | solution.py:221
  32.0 9.4 %all_to_all.11 = f32[16,16,128]{2,1,0:T(8,128)S(1)} all-to-all(f32[16,16,128]{2,1,0:T(8,128)S(1)} %bitcast.14), channel_id=1, replica_groups=mesh['ta'=2,'z'=4,'y'=4,'x'=4] {'y','x'}, dimensions={0} | all-to-all | bytes 262144 | tf_op jit(solution)/shard_map/all_to_all | solution.py:230
  41.4 3.2 %collective-permute-start.1 = (f32[16,128]{1,0:T(8,128)S(1)}, f32[16,128]{1,0:T(8,128)S(1)}, u32[]{:S(2)}, u32[]{:S(2)}) collective-permute-start(f32[16,128]{1,0:T(8,128)S(1)} %reduce_sum.9), channel_id=1, source_target_pairs={{0,64},{64,0},{1,65},{65,1},{2,66},{66,2},{3,67},{67,3},{4,68},{68... | collective-permute-start | bytes 24584 | tf_op jit(solution)/shard_map/ppermute | solution.py:234
  44.7 0.8 %collective-permute-done.1 = f32[16,128]{1,0:T(8,128)S(1)} collective-permute-done((f32[16,128]{1,0:T(8,128)S(1)}, f32[16,128]{1,0:T(8,128)S(1)}, u32[]{:S(2)}, u32[]{:S(2)}) %collective-permute-start.1) | collective-permute-done | bytes 8224 | tf_op jit(solution)/shard_map/ppermute | solution.py:234
  45.5 0.6 %maximum_multiply_fusion = f32[6,193]{1,0:T(8,128)} fusion(f32[6,65]{1,0:T(8,128)S(1)} %slice.9, f32[6,128]{1,0:T(8,128)S(1)} %slice.8), kind=kLoop, calls=%fused_computation | loop fusion | flops 2316 | bytes 9264 | tf_op jit(solution)/shard_map/div | solution.py:235
  (4 shorter events, 0.0 us)
Async XLA Ops:
  2.7 3.6 %collective-permute-start = (f32[12,6,18,128]{3,2,1,0:T(8,128)S(1)}, f32[12,6,18,128]{3,2,1,0:T(8,128)S(1)}, u32[]{:S(2)}, u32[]{:S(2)}) collective-permute-start(f32[12,6,18,128]{3,2,1,0:T(8,128)S(1)} %product_sent.1), channel_id=1, source_target_pairs={{0,64},{64,0},{1,65},{65,1},{2,66},{66,2},{3,67},{67,3},{4,68},{68... | collective-permute-start | bytes 1990664 | tf_op jit(solution)/shard_map/ppermute | solution.py:201
  41.4 4.1 %collective-permute-start.1 = (f32[16,128]{1,0:T(8,128)S(1)}, f32[16,128]{1,0:T(8,128)S(1)}, u32[]{:S(2)}, u32[]{:S(2)}) collective-permute-start(f32[16,128]{1,0:T(8,128)S(1)} %reduce_sum.9), channel_id=1, source_target_pairs={{0,64},{64,0},{1,65},{65,1},{2,66},{66,2},{3,67},{67,3},{4,68},{68... | collective-permute-start | bytes 24584 | tf_op jit(solution)/shard_map/ppermute | solution.py:234

commit v3 on v2

v3 whole, which is shorter than its diff:
```python
import functools

import jax
import jax.numpy as jnp
from jax import lax
from jax.experimental import pallas as pl
from jax.experimental.layout import Layout, with_layout_constraint
from jax.experimental.pallas import tpu as pltpu
from jax.sharding import Mesh, PartitionSpec as P

F32 = jnp.float32
LANES = 128
WIDE = pltpu.CompilerParams(vmem_limit_bytes=50 * 2**20)
SMALL = pltpu.CompilerParams(vmem_limit_bytes=12 * 2**20)


def cross_conj(first, second):
    row = []
    for k in range(3):
        a, b = (k + 1) % 3, (k + 2) % 3
        (fa, ga), (fb, gb) = first[a], first[b]
        (sa, ta), (sb, tb) = second[a], second[b]
        real = (fa * sb - ga * tb) - (fb * sa - gb * ta)
        imag = (fb * ta + gb * sa) - (fa * tb + ga * sb)
        row.append((real, imag))
    return row


def rows_times(rows, matrix):
    out = []
    for row in rows:
        line = []
        for j in range(3):
            real = imag = None
            for m in range(3):
                (ar, ai), (br, bi) = row[m], matrix[m][j]
                re = ar * br - ai * bi
                im = ar * bi + ai * br
                real = re if real is None else real + re
                imag = im if imag is None else imag + im
            line.append((real, imag))
        out.append(line)
    return out


THIRD = 1.0 / 3.0
MSG = 14
RES = 10
CHUNKS = ((0, 8), (8, 8), (16, 2))


def half_reads(half, links_ref, links, sems):
    copies = []
    for x in range(6):
        source = pl.ds(pl.multiple_of(72 * x + 32 * half, 8), 40)
        copies.append(
            pltpu.make_async_copy(
                links_ref.at[:, pl.ds(0, 2), :, source, :], links.at[x], sems.at[x, 0]
            )
        )
    return copies


def multiply_half(half, links, out_ref, x):
    for start, count in CHUNKS:
        def load(t, i, j):
            return tuple(
                links[x, t, i, j, pl.ds(4 * half + 2 * start + c, count, stride=2), :]
                for c in range(2)
            )

        rows = [[load(0, i, j) for j in range(3)] for i in range(2)]
        for t in (1, 2):
            matrix = [[load(t, i, j) for j in range(3)] for i in range(2)]
            matrix.append(cross_conj(matrix[0], matrix[1]))
            rows = rows_times(rows, matrix)
        if out_ref.shape[0] == 18:
            rows.append(cross_conj(rows[0], rows[1]))
            rows = [[(re * THIRD, im * THIRD) for re, im in row] for row in rows]
        for i, row in enumerate(rows):
            for j in range(3):
                for c in range(2):
                    out_ref[6 * i + 2 * j + c, pl.ds(18 * x + start, count), :] = row[j][c]


def product_kernel(other, links_ref, out_ref, links, sems):
    half = lax.axis_index("ta")
    half = 1 - half if other else half
    copies = half_reads(half, links_ref, links, sems)
    for copy in copies:
        copy.start()
    for x in range(6):
        for copy in copies[x : x + 1]:
            copy.wait()
        multiply_half(half, links, out_ref, x)


def product(links, other):
    return pl.pallas_call(
        functools.partial(product_kernel, other),
        in_specs=[pl.BlockSpec(memory_space=pltpu.HBM)],
        out_specs=pl.BlockSpec(memory_space=pltpu.VMEM),
        out_shape=jax.ShapeDtypeStruct((12 if other else 18, 108, LANES), F32),
        scratch_shapes=[
            pltpu.VMEM((6, 3, 2, 3, 40, LANES), F32),
            pltpu.SemaphoreType.DMA((6, 3)),
        ],
        compiler_params=WIDE,
        cost_estimate=pl.CostEstimate(
            flops=40_000_000, bytes_accessed=2_000_000, transcendentals=0
        ),
        name="product_sent" if other else "product_kept",
    )(links)


def trace_kernel(keep_ref, got_ref, planes_ref, msg_ref):
    for start in range(0, 108, 8):
        count = min(8, 108 - start)

        def load(ref, rows):
            return [
                [
                    tuple(ref[6 * i + 2 * j + c, pl.ds(start, count), :] for c in range(2))
                    for j in range(3)
                ]
                for i in range(rows)
            ]

        own, other = load(keep_ref, 3), load(got_ref, 2)
        other.append(cross_conj(other[0], other[1]))
        real = imag = None
        for i in range(3):
            for j in range(3):
                (ar, ai), (br, bi) = own[i][j], other[j][i]
                re = ar * br - ai * bi
                im = ar * bi + ai * br
                real = re if real is None else real + re
                imag = im if imag is None else imag + im
        planes_ref[pl.ds(2 * start, count, stride=2), :] = real
        planes_ref[pl.ds(2 * start + 1, count, stride=2), :] = imag
    lane = lax.broadcasted_iota(jnp.int32, (4, LANES), 1) // 32
    tails = []
    for p in range(6):
        for c in range(2):
            for slot in range(2):
                count = 9 if c == 0 else 7
                tiles = planes_ref[pl.ds(36 * p + 2 * slot + c, count, stride=4), :]
                msg_ref[0, pl.ds(MSG * 9 * c + 6 * slot + p, count, stride=MSG), :] = tiles
        tails.append(planes_ref[pl.ds(36 * p + 28 + 1, 4, stride=2), :])
    for b in range(4):
        for row, members in ((12, (0, 1, 2, 3)), (13, (4, 5))):
            packed = jnp.zeros((4, LANES), F32)
            for place, p in enumerate(members):
                shift = (32 * (place - b)) % LANES
                moved = pltpu.roll(tails[p], shift, 1) if shift else tails[p]
                packed = jnp.where(lane == place, moved, packed)
            msg_ref[0, pl.ds(MSG * b + row, 4, stride=4 * MSG), :] = packed
    for z in range(1, 4):
        msg_ref[z] = msg_ref[0]


def dot_rows(left, right):
    return lax.dot_general(
        left, right, (((1,), (1,)), ((), ())), preferred_element_type=F32
    )


def correlate_kernel(got_ref, planes_ref, out_ref, result_ref, rows_ref, shift_ref, sem):
    write = pltpu.make_async_copy(planes_ref, result_ref, sem)
    write.start()
    mine = lax.axis_index("z")

    @pl.when(mine < 4)
    def _():
        correlate(mine, got_ref, out_ref, rows_ref, shift_ref)

    write.wait()


def correlate(mine, got_ref, out_ref, rows_ref, shift_ref):
    lane = lax.broadcasted_iota(jnp.int32, (16, LANES), 1)
    for z in range(3):
        block = (mine + z) % 4
        for p in range(6):
            target = pl.ds(96 * z + p, 16, stride=6)
            for k in range(2):
                rows_ref[k, target, :] = got_ref[block, pl.ds(6 * k + p, 16, stride=MSG), :]
            tail = got_ref[block, pl.ds(12 + p // 4, 16, stride=MSG), :]
            shift = (-32 * (p % 4)) % LANES
            tail = pltpu.roll(tail, shift, 1) if shift else tail
            rows_ref[2, target, :] = jnp.where(lane < 32, tail, 0.0)
    rows = jnp.concatenate([rows_ref[k] for k in range(3)], axis=1)
    high = rows.astype(jnp.bfloat16)
    low = (rows - high.astype(F32)).astype(jnp.bfloat16)
    both = dot_rows(jnp.concatenate([high[:96], low[:96]], axis=0), high)
    products = both[:96] + (both[96:] + dot_rows(high[:96], low))
    products = jnp.concatenate([products, jnp.zeros((96, 96), F32)], axis=1)
    row = lax.broadcasted_iota(jnp.int32, (96, 384), 0)
    for bit in (1, 2, 4):
        products = jnp.where((row & bit) != 0, pltpu.roll(products, 384 - bit, 1), products)
    for g in range(12):
        group = products[8 * g : 8 * g + 8]
        if g:
            group = pltpu.roll(group, 384 - 8 * g, 1)
        for k in range(2):
            shift_ref[k, pl.ds(8 * g, 8), :] = group[:, LANES * k : LANES * (k + 1)]
    far = []
    for p in range(6):
        out_ref[0, pl.ds(p, 16, stride=RES), :] = shift_ref[0, pl.ds(p, 16, stride=6), :]
        far.append(shift_ref[1, pl.ds(p, 16, stride=6), :])
    last = jnp.zeros((16, LANES), F32)
    for p in range(6):
        last = jnp.where(lane == p, pltpu.roll(far[p], 64 + p, 1), last)
    out_ref[0, pl.ds(9, 16, stride=RES), :] = last
    for q in range(3):
        pair = jnp.where(lane < 64, far[2 * q], pltpu.roll(far[2 * q + 1], 64, 1))
        out_ref[0, pl.ds(6 + q, 16, stride=RES), :] = pair
    out_ref[1] = out_ref[0]


def total_kernel(pieces_ref, out_ref):
    sums = [
        jnp.sum(pieces_ref[pl.ds(k, 32, stride=RES), :], axis=0, keepdims=True) * (1.0 / 4608.0)
        for k in range(RES)
    ]
    lane = lax.broadcasted_iota(jnp.int32, (1, LANES), 1)
    for p in range(6):
        out_ref[pl.ds(p, 1), pl.ds(0, LANES)] = sums[p]
        far = sums[6 + p // 2]
        far = pltpu.roll(far, 64, 1) if p % 2 else far
        far = jnp.where(lane < 64, far, pltpu.roll(sums[9], 64 - p, 1))
        out_ref[pl.ds(p, 1), pl.ds(LANES, 65)] = far[:, :65]


def vmem(count):
    return [pl.BlockSpec(memory_space=pltpu.VMEM)] * count


def per_device(time_links):
    links = with_layout_constraint(
        time_links.reshape(3, 2, 3, 3, 6, 36, LANES),
        Layout((0, 2, 3, 4, 5, 1, 6)),
    )
    links = jnp.transpose(links, (0, 2, 3, 4, 5, 1, 6)).reshape(3, 3, 3, 432, LANES)
    got = lax.ppermute(product(links, True), "ta", [(0, 1), (1, 0)])
    keep = product(links, False)
    planes, messages = pl.pallas_call(
        trace_kernel,
        in_specs=vmem(2),
        out_specs=vmem(2),
        out_shape=[
            jax.ShapeDtypeStruct((216, LANES), F32),
            jax.ShapeDtypeStruct((4, 16 * MSG, LANES), F32),
        ],
        compiler_params=SMALL,
        name="trace",
    )(keep, got)
    gathered = exchange(messages, ("z", "y", "x"), MSG)
    partial, planes = pl.pallas_call(
        correlate_kernel,
        in_specs=vmem(2),
        out_specs=vmem(1) + [pl.BlockSpec(memory_space=pltpu.HBM)],
        out_shape=[
            jax.ShapeDtypeStruct((2, 16 * RES, LANES), F32),
            jax.ShapeDtypeStruct((216, LANES), F32),
        ],
        scratch_shapes=[
            pltpu.VMEM((3, 288, LANES), F32),
            pltpu.VMEM((2, 96, LANES), F32),
            pltpu.SemaphoreType.DMA,
        ],
        compiler_params=SMALL,
        name="correlate",
    )(gathered, planes)
    loop_planes = with_layout_constraint(
        planes.reshape(6, 18, 2, LANES).transpose(0, 2, 1, 3),
        Layout((0, 2, 1, 3)),
    ).reshape(6, 2, 2304)
    pieces = exchange(partial, ("ta", "y", "x"), RES)
    correlator = pl.pallas_call(
        total_kernel,
        in_specs=vmem(1),
        out_specs=pl.BlockSpec(memory_space=pltpu.VMEM),
        out_shape=jax.ShapeDtypeStruct((6, 193), F32),
        compiler_params=SMALL,
        name="total",
    )(pieces.reshape(32 * RES, LANES))
    return loop_planes, correlator


def exchange(values, axes, rows):
    shape = values.shape
    values = values.reshape(-1, rows // 2, 2, LANES)
    return lax.all_to_all(values, axes, split_axis=0, concat_axis=0, tiled=True).reshape(shape)


def solution(mesh):
    grid = Mesh(mesh.devices.reshape(2, 4, 4, 4), ("ta", "z", "y", "x"))
    gx = ("z", "y", "x")
    return jax.shard_map(
        per_device,
        mesh=grid,
        in_specs=(P("ta", None, None, None, gx, None),),
        out_specs=(P(gx, None, "ta"), P(gx, None)),
        check_vma=False,
    )
```

time: 46.4 us -> 43.7 us (0.942)
  starting transfers between devices: 4.7 us -> 1.46 us
  blocking collectives: 33 us -> 35.4 us
  waiting for transfers between devices: 0.83 us -> 0.01 us
  other arithmetic: 0.63 us -> 0 us
    ppermute x1 -> x0, starting transfers between devices: 3.24 us -> none  [per_device(): total = total + lax.ppermute(total, 'ta', [(0, 1), (1, 0)])]
    all_to_all x2, blocking collectives: 33 us -> 35.4 us  [exchange(): lax.all_to_all(values, axes, split_axis=0, concat_axis=0, tiled=True)]
    ppermute x1 -> x0, waiting for transfers between devices: 0.83 us -> none  [per_device(): total = total + lax.ppermute(total, 'ta', [(0, 1), (1, 0)])]
    pallas_call x1, Pallas kernels: 1.08 us -> 0.27 us  [per_device(): pl.pallas_call(trace_kernel, in_specs=vmem(2), out_specs=vmem(2), out_sha...]
    div x1 -> x0, other arithmetic: 0.61 us -> none  [per_device(): jnp.concatenate([total[0:6], total[8:14, :65]], axis=1) / 4608.0]
    pallas_call x1 -> x2, Pallas kernels: 1.01 us -> 1.46 us  [the longest x1 0.78 us: per_device(): pl.pallas_call(correlate_kernel, in_specs=vmem(2), out_specs=vmem(1) + [p...]
  transfers between devices with their start and end apart: 2 -> 1, of which waited for: 1 -> 0; matrix products, arithmetic and copies ran while one was open for 0% -> 0% of each run, Pallas kernels for 5% -> 5%
where the time goes in v3:
time: 43.7 us; the launch traced here: 43.4 us
  blocking collectives  35.4 us (81%)
  Pallas kernels  5.91 us (14%)
  starting transfers between devices  1.46 us (3%)
  between operations  0.67 us (2%)
    all_to_all x2, blocking collectives, exchange(): lax.all_to_all(values, axes, split_axis=0, concat_axis=0, tiled=True)  35.4 us
    pallas_call x2, Pallas kernels, product(): pl.pallas_call(functools.partial(product_kernel, other), in_specs=[pl.Blo...  4.17 us
    ppermute x1, starting transfers between devices, per_device(): got = lax.ppermute(product(links, True), 'ta', [(0, 1), (1, 0)])  1.46 us
  transfers between devices with their start and end apart: 1, of which 0 were waited for; matrix products, arithmetic and copies ran while one was open for 0% of the time, Pallas kernels for 5%

profile of v3, /device:TPU:1, one launch (start us, length us, event | category | flops | bytes accessed | tf_op | source)
XLA Modules:
  0.0 43.4 jit_solution(15248155817430235456)
XLA Ops:
  0.6 2.0 %product_sent.1 = f32[12,108,128]{2,1,0:T(8,128)S(1)} custom-call(f32[3,3,3,432,128]{4,3,2,1,0:T(8,128)} %bitcast.18), custom_call_target="tpu_custom_call" | custom-call | flops 40000000 | bytes 2000000 | tf_op jit(solution)/shard_map/product_sent/pallas_call | solution.py:99
  2.7 1.5 %collective-permute-start = (f32[12,108,128]{2,1,0:T(8,128)S(1)}, f32[12,108,128]{2,1,0:T(8,128)S(1)}, u32[]{:S(2)}, u32[]{:S(2)}) collective-permute-start(f32[12,108,128]{2,1,0:T(8,128)S(1)} %product_sent.1), channel_id=1, source_target_pairs={{0,64},{64,0},{1,65},{65,1},{2,66},{66,2},{3,67},{67,3},{4,68},{68... | collective-permute-start | bytes 1990664 | tf_op jit(solution)/shard_map/ppermute | solution.py:245
  4.1 2.1 %product_kept.1.keep_ref = f32[18,108,128]{2,1,0:T(8,128)S(1)} custom-call(f32[3,3,3,432,128]{4,3,2,1,0:T(8,128)} %bitcast.19), custom_call_target="tpu_custom_call" | custom-call | flops 40000000 | bytes 2000000 | tf_op jit(solution)/shard_map/product_kept/pallas_call | solution.py:99
  6.3 0.0 collective-permute-done.got_ref
  6.3 0.3 trace.1
  6.6 23.2 %all_to_all.10 = f32[64,7,2,128]{3,2,1,0:T(2,128)S(1)} all-to-all(f32[64,7,2,128]{3,2,1,0:T(2,128)S(1)} %bitcast.16), channel_id=1, replica_groups=mesh['ta'=2,'z'=4,'y'=4,'x'=4] {'z','y','x'}, dimensions={0} | all-to-all | bytes 917504 | tf_op jit(solution)/shard_map/all_to_all | solution.py:294
  29.7 0.8 %correlate.1 = (f32[2,160,128]{2,1,0:T(8,128)S(1)}, f32[216,128]{1,0:T(8,128)}) custom-call(f32[4,224,128]{2,1,0:T(8,128)S(1)} %bitcast.14, f32[216,128]{1,0:T(8,128)S(1)} %get-tuple-element.7.planes_ref), custom_call_target="tpu_custom_call" | custom-call | tf_op jit(solution)/shard_map/correlate/pallas_call | solution.py:259
  30.5 12.2 %all_to_all.11 = f32[32,5,2,128]{3,2,1,0:T(2,128)S(1)} all-to-all(f32[32,5,2,128]{3,2,1,0:T(2,128)S(1)} %bitcast.17), channel_id=1, replica_groups=mesh['ta'=2,'z'=4,'y'=4,'x'=4] {'ta','y','x'}, dimensions={0} | all-to-all | bytes 327680 | tf_op jit(solution)/shard_map/all_to_all | solution.py:294
  42.7 0.7 %total.1 = f32[6,193]{1,0:T(8,128)} custom-call(f32[320,128]{1,0:T(8,128)S(1)} %bitcast.15), custom_call_target="tpu_custom_call" | custom-call | tf_op jit(solution)/shard_map/total/pallas_call | solution.py:280
Async XLA Ops:
  2.7 3.6 %collective-permute-start = (f32[12,108,128]{2,1,0:T(8,128)S(1)}, f32[12,108,128]{2,1,0:T(8,128)S(1)}, u32[]{:S(2)}, u32[]{:S(2)}) collective-permute-start(f32[12,108,128]{2,1,0:T(8,128)S(1)} %product_sent.1), channel_id=1, source_target_pairs={{0,64},{64,0},{1,65},{65,1},{2,66},{66,2},{3,67},{67,3},{4,68},{68... | collective-permute-start | bytes 1990664 | tf_op jit(solution)/shard_map/ppermute | solution.py:245

commit v4 on v3

--- a/solution.py
+++ b/solution.py
@@ -49,23 +49,23 @@
 CHUNKS = ((0, 8), (8, 8), (16, 2))
 
 
-def half_reads(half, links_ref, links, sems):
+def half_reads(half, links_ref, links, sems, planes=range(6)):
     copies = []
-    for x in range(6):
+    for i, x in enumerate(planes):
         source = pl.ds(pl.multiple_of(72 * x + 32 * half, 8), 40)
         copies.append(
             pltpu.make_async_copy(
-                links_ref.at[:, pl.ds(0, 2), :, source, :], links.at[x], sems.at[x, 0]
+                links_ref.at[:, pl.ds(0, 2), :, source, :], links.at[i], sems.at[i]
             )
         )
     return copies
 
 
-def multiply_half(half, links, out_ref, x):
+def multiply_half(half, links, out_ref, x, place):
     for start, count in CHUNKS:
         def load(t, i, j):
             return tuple(
-                links[x, t, i, j, pl.ds(4 * half + 2 * start + c, count, stride=2), :]
+                links[place, t, i, j, pl.ds(4 * half + 2 * start + c, count, stride=2), :]
                 for c in range(2)
             )
 
@@ -83,34 +83,69 @@
                     out_ref[6 * i + 2 * j + c, pl.ds(18 * x + start, count), :] = row[j][c]
 
 
-def product_kernel(other, links_ref, out_ref, links, sems):
-    half = lax.axis_index("ta")
-    half = 1 - half if other else half
-    copies = half_reads(half, links_ref, links, sems)
+EARLY = 2
+
+
+def sent_kernel(links_ref, out_ref, early, links, sems, early_sems):
+    mine = lax.axis_index("ta")
+    copies = half_reads(1 - mine, links_ref, links, sems)
+    ahead = half_reads(mine, links_ref, early, early_sems, range(EARLY))
+    for copy in copies + ahead:
+        copy.start()
+    for x in range(6):
+        copies[x].wait()
+        multiply_half(1 - mine, links, out_ref, x, x)
+    for copy in ahead:
+        copy.wait()
+
+
+def kept_kernel(links_ref, early, out_ref, links, sems):
+    mine = lax.axis_index("ta")
+    copies = half_reads(mine, links_ref, links, sems, range(EARLY, 6))
     for copy in copies:
         copy.start()
-    for x in range(6):
-        for copy in copies[x : x + 1]:
-            copy.wait()
-        multiply_half(half, links, out_ref, x)
-
-
-def product(links, other):
-    return pl.pallas_call(
-        functools.partial(product_kernel, other),
-        in_specs=[pl.BlockSpec(memory_space=pltpu.HBM)],
-        out_specs=pl.BlockSpec(memory_space=pltpu.VMEM),
-        out_shape=jax.ShapeDtypeStruct((12 if other else 18, 108, LANES), F32),
+    for x in range(EARLY):
+        multiply_half(mine, early, out_ref, x, x)
+    for x in range(EARLY, 6):
+        copies[x - EARLY].wait()
+        multiply_half(mine, links, out_ref, x, x - EARLY)
+
+
+def product(links):
+    hbm = [pl.BlockSpec(memory_space=pltpu.HBM)]
+    cost = pl.CostEstimate(flops=40_000_000, bytes_accessed=2_000_000, transcendentals=0)
+    sent, early = pl.pallas_call(
+        sent_kernel,
+        in_specs=hbm,
+        out_specs=vmem(2),
+        out_shape=[
+            jax.ShapeDtypeStruct((12, 108, LANES), F32),
+            jax.ShapeDtypeStruct((EARLY, 3, 2, 3, 40, LANES), F32),
+        ],
         scratch_shapes=[
             pltpu.VMEM((6, 3, 2, 3, 40, LANES), F32),
-            pltpu.SemaphoreType.DMA((6, 3)),
+            pltpu.SemaphoreType.DMA((6,)),
+            pltpu.SemaphoreType.DMA((EARLY,)),
         ],
         compiler_params=WIDE,
-        cost_estimate=pl.CostEstimate(
-            flops=40_000_000, bytes_accessed=2_000_000, transcendentals=0
-        ),
-        name="product_sent" if other else "product_kept",
+        cost_estimate=cost,
+        name="product_sent",
     )(links)
+    got = lax.ppermute(sent, "ta", [(0, 1), (1, 0)])
+    keep = pl.pallas_call(
+        kept_kernel,
+        in_specs=hbm + vmem(1),
+        out_specs=pl.BlockSpec(memory_space=pltpu.VMEM),
+        out_shape=jax.ShapeDtypeStruct((18, 108, LANES), F32),
+        scratch_shapes=[
+            pltpu.VMEM((6 - EARLY, 3, 2, 3, 40, LANES), F32),
+            pltpu.SemaphoreType.DMA((6 - EARLY,)),
+        ],
+        compiler_params=WIDE,
+        cost_estimate=cost,
+        name="product_kept",
+    )(links, early)
+    return keep, got
 
 
 def trace_kernel(keep_ref, got_ref, planes_ref, msg_ref):
@@ -242,8 +277,7 @@
         Layout((0, 2, 3, 4, 5, 1, 6)),
     )
     links = jnp.transpose(links, (0, 2, 3, 4, 5, 1, 6)).reshape(3, 3, 3, 432, LANES)
-    got = lax.ppermute(product(links, True), "ta", [(0, 1), (1, 0)])
-    keep = product(links, False)
+    keep, got = product(links)
     planes, messages = pl.pallas_call(
         trace_kernel,
         in_specs=vmem(2),

time: 43.7 us -> 43.2 us (0.989)
  Pallas kernels: 5.91 us -> 5.36 us
    pallas_call x2, Pallas kernels: 4.17 us -> 3.63 us  [the longest x1 1.94 us: product(): pl.pallas_call(sent_kernel, in_specs=hbm, out_specs=vmem(2), out_shape=[j...]
  transfers between devices with their start and end apart: 1 -> 1, of which waited for: 0 -> 1; matrix products, arithmetic and copies ran while one was open for 0% -> 0% of each run, Pallas kernels for 5% -> 4%
where the time goes in v4:
time: 43.2 us; the launch traced here: 42.9 us
  blocking collectives  35.4 us (82%)
  Pallas kernels  5.36 us (12%)
  starting transfers between devices  1.46 us (3%)
  between operations  0.66 us (2%)
    all_to_all x2, blocking collectives, exchange(): lax.all_to_all(values, axes, split_axis=0, concat_axis=0, tiled=True)  35.4 us
    pallas_call x1, Pallas kernels, product(): pl.pallas_call(sent_kernel, in_specs=hbm, out_specs=vmem(2), out_shape=[j...  1.94 us
    pallas_call x1, Pallas kernels, product(): pl.pallas_call(kept_kernel, in_specs=hbm + vmem(1), out_specs=pl.BlockSpe...  1.69 us
    ppermute x1, starting transfers between devices, product(): got = lax.ppermute(sent, 'ta', [(0, 1), (1, 0)])  1.46 us
  transfers between devices with their start and end apart: 1, of which 1 were waited for; matrix products, arithmetic and copies ran while one was open for 0% of the time, Pallas kernels for 4%

profile of v4, /device:TPU:1, one launch (start us, length us, event | category | flops | bytes accessed | tf_op | source)
XLA Modules:
  0.0 42.9 jit_solution(3213155023537891373)
XLA Ops:
  0.6 1.9 %product_sent.1 = (f32[12,108,128]{2,1,0:T(8,128)S(1)}, f32[2,3,2,3,40,128]{5,4,3,2,1,0:T(8,128)S(1)}) custom-call(f32[3,3,3,432,128]{4,3,2,1,0:T(8,128)} %bitcast.18), custom_call_target="tpu_custom_call" | custom-call | flops 40000000 | bytes 2000000 | tf_op jit(solution)/shard_map/product_sent/pallas_call | solution.py:117
  2.6 1.5 %collective-permute-start = (f32[12,108,128]{2,1,0:T(8,128)S(1)}, f32[12,108,128]{2,1,0:T(8,128)S(1)}, u32[]{:S(2)}, u32[]{:S(2)}) collective-permute-start(f32[12,108,128]{2,1,0:T(8,128)S(1)} %get-tuple-element.9), channel_id=1, source_target_pairs={{0,64},{64,0},{1,65},{65,1},{2,66},{66,2},{3,67},{67,3},{4,68},{68... | collective-permute-start | bytes 1990664 | tf_op jit(solution)/shard_map/ppermute | solution.py:134
  4.0 1.7 %product_kept.1.keep_ref = f32[18,108,128]{2,1,0:T(8,128)S(1)} custom-call(f32[3,3,3,432,128]{4,3,2,1,0:T(8,128)} %bitcast.19, f32[2,3,2,3,40,128]{5,4,3,2,1,0:T(8,128)S(1)} %get-tuple-element.8.early), custom_call_target="tpu_custom_call" | custom-call | flops 40000000 | bytes 2000000 | tf_op jit(solution)/shard_map/product_kept/pallas_call | solution.py:135
  5.7 0.1 collective-permute-done.got_ref
  5.8 0.3 trace.1
  6.1 22.9 %all_to_all.10 = f32[64,7,2,128]{3,2,1,0:T(2,128)S(1)} all-to-all(f32[64,7,2,128]{3,2,1,0:T(2,128)S(1)} %bitcast.16), channel_id=1, replica_groups=mesh['ta'=2,'z'=4,'y'=4,'x'=4] {'z','y','x'}, dimensions={0} | all-to-all | bytes 917504 | tf_op jit(solution)/shard_map/all_to_all | solution.py:328
  29.0 0.8 %correlate.1 = (f32[2,160,128]{2,1,0:T(8,128)S(1)}, f32[216,128]{1,0:T(8,128)}) custom-call(f32[4,224,128]{2,1,0:T(8,128)S(1)} %bitcast.14, f32[216,128]{1,0:T(8,128)S(1)} %get-tuple-element.11.planes_ref), custom_call_target="tpu_custom_call" | custom-call | tf_op jit(solution)/shard_map/correlate/pallas_call | solution.py:293
  29.8 12.5 %all_to_all.11 = f32[32,5,2,128]{3,2,1,0:T(2,128)S(1)} all-to-all(f32[32,5,2,128]{3,2,1,0:T(2,128)S(1)} %bitcast.17), channel_id=1, replica_groups=mesh['ta'=2,'z'=4,'y'=4,'x'=4] {'ta','y','x'}, dimensions={0} | all-to-all | bytes 327680 | tf_op jit(solution)/shard_map/all_to_all | solution.py:328
  42.3 0.7 %total.1 = f32[6,193]{1,0:T(8,128)} custom-call(f32[320,128]{1,0:T(8,128)S(1)} %bitcast.15), custom_call_target="tpu_custom_call" | custom-call | tf_op jit(solution)/shard_map/total/pallas_call | solution.py:314
Async XLA Ops:
  2.6 3.2 %collective-permute-start = (f32[12,108,128]{2,1,0:T(8,128)S(1)}, f32[12,108,128]{2,1,0:T(8,128)S(1)}, u32[]{:S(2)}, u32[]{:S(2)}) collective-permute-start(f32[12,108,128]{2,1,0:T(8,128)S(1)} %get-tuple-element.9), channel_id=1, source_target_pairs={{0,64},{64,0},{1,65},{65,1},{2,66},{66,2},{3,67},{67,3},{4,68},{68... | collective-permute-start | bytes 1990664 | tf_op jit(solution)/shard_map/ppermute | solution.py:134

commit v5 on v4

--- a/solution.py
+++ b/solution.py
@@ -44,7 +44,7 @@
 
 
 THIRD = 1.0 / 3.0
-MSG = 14
+MSG = 7
 RES = 10
 CHUNKS = ((0, 8), (8, 8), (16, 2))
 
@@ -173,25 +173,22 @@
                 imag = im if imag is None else imag + im
         planes_ref[pl.ds(2 * start, count, stride=2), :] = real
         planes_ref[pl.ds(2 * start + 1, count, stride=2), :] = imag
-    lane = lax.broadcasted_iota(jnp.int32, (4, LANES), 1) // 32
+    lane = lax.broadcasted_iota(jnp.int32, (4, LANES), 1) // 16
     tails = []
     for p in range(6):
         for c in range(2):
-            for slot in range(2):
-                count = 9 if c == 0 else 7
-                tiles = planes_ref[pl.ds(36 * p + 2 * slot + c, count, stride=4), :]
-                msg_ref[0, pl.ds(MSG * 9 * c + 6 * slot + p, count, stride=MSG), :] = tiles
+            count = 18 if c == 0 else 14
+            tiles = planes_ref[pl.ds(36 * p + c, count, stride=2), :]
+            msg_ref[0, pl.ds(MSG * 18 * c + p, count, stride=MSG), :] = tiles
         tails.append(planes_ref[pl.ds(36 * p + 28 + 1, 4, stride=2), :])
-    for b in range(4):
-        for row, members in ((12, (0, 1, 2, 3)), (13, (4, 5))):
-            packed = jnp.zeros((4, LANES), F32)
-            for place, p in enumerate(members):
-                shift = (32 * (place - b)) % LANES
-                moved = pltpu.roll(tails[p], shift, 1) if shift else tails[p]
-                packed = jnp.where(lane == place, moved, packed)
-            msg_ref[0, pl.ds(MSG * b + row, 4, stride=4 * MSG), :] = packed
-    for z in range(1, 4):
-        msg_ref[z] = msg_ref[0]
+    for b in range(8):
+        packed = jnp.zeros((4, LANES), F32)
+        for p in range(6):
+            shift = (16 * (p - b)) % LANES
+            moved = pltpu.roll(tails[p], shift, 1) if shift else tails[p]
+            packed = jnp.where(lane == p, moved, packed)
+        msg_ref[0, pl.ds(MSG * b + 6, 4, stride=8 * MSG), :] = packed
+    msg_ref[1] = msg_ref[0]
 
 
 def dot_rows(left, right):
@@ -203,9 +200,9 @@
 def correlate_kernel(got_ref, planes_ref, out_ref, result_ref, rows_ref, shift_ref, sem):
     write = pltpu.make_async_copy(planes_ref, result_ref, sem)
     write.start()
-    mine = lax.axis_index("z")
-
-    @pl.when(mine < 4)
+    mine = lax.axis_index("zh")
+
+    @pl.when(mine < 2)
     def _():
         correlate(mine, got_ref, out_ref, rows_ref, shift_ref)
 
@@ -214,43 +211,40 @@
 
 def correlate(mine, got_ref, out_ref, rows_ref, shift_ref):
     lane = lax.broadcasted_iota(jnp.int32, (16, LANES), 1)
-    for z in range(3):
-        block = (mine + z) % 4
+    for z in range(4):
+        block = (2 * mine + z) % 4
+        tails = got_ref[block, pl.ds(6, 16, stride=MSG), :]
         for p in range(6):
             target = pl.ds(96 * z + p, 16, stride=6)
-            for k in range(2):
-                rows_ref[k, target, :] = got_ref[block, pl.ds(6 * k + p, 16, stride=MSG), :]
-            tail = got_ref[block, pl.ds(12 + p // 4, 16, stride=MSG), :]
-            shift = (-32 * (p % 4)) % LANES
-            tail = pltpu.roll(tail, shift, 1) if shift else tail
-            rows_ref[2, target, :] = jnp.where(lane < 32, tail, 0.0)
-    rows = jnp.concatenate([rows_ref[k] for k in range(3)], axis=1)
+            rows_ref[0, target, :] = got_ref[block, pl.ds(p, 16, stride=MSG), :]
+            tail = pltpu.roll(tails, LANES - 16 * p, 1) if p else tails
+            rows_ref[1, target, :] = jnp.where(lane < 16, tail, 0.0)
+    rows = jnp.concatenate([rows_ref[k] for k in range(2)], axis=1)
     high = rows.astype(jnp.bfloat16)
     low = (rows - high.astype(F32)).astype(jnp.bfloat16)
-    both = dot_rows(jnp.concatenate([high[:96], low[:96]], axis=0), high)
-    products = both[:96] + (both[96:] + dot_rows(high[:96], low))
-    products = jnp.concatenate([products, jnp.zeros((96, 96), F32)], axis=1)
-    row = lax.broadcasted_iota(jnp.int32, (96, 384), 0)
+    both = dot_rows(jnp.concatenate([high[:192], low[:192]], axis=0), high)
+    products = both[:192] + (both[192:] + dot_rows(high[:192], low))
+    row = lax.broadcasted_iota(jnp.int32, (192, 384), 0)
     for bit in (1, 2, 4):
         products = jnp.where((row & bit) != 0, pltpu.roll(products, 384 - bit, 1), products)
-    for g in range(12):
+    for g in range(24):
         group = products[8 * g : 8 * g + 8]
         if g:
             group = pltpu.roll(group, 384 - 8 * g, 1)
         for k in range(2):
             shift_ref[k, pl.ds(8 * g, 8), :] = group[:, LANES * k : LANES * (k + 1)]
+    lane = lax.broadcasted_iota(jnp.int32, (32, LANES), 1)
     far = []
     for p in range(6):
-        out_ref[0, pl.ds(p, 16, stride=RES), :] = shift_ref[0, pl.ds(p, 16, stride=6), :]
-        far.append(shift_ref[1, pl.ds(p, 16, stride=6), :])
-    last = jnp.zeros((16, LANES), F32)
+        out_ref[pl.ds(p, 32, stride=RES), :] = shift_ref[0, pl.ds(p, 32, stride=6), :]
+        far.append(shift_ref[1, pl.ds(p, 32, stride=6), :])
+    last = jnp.zeros((32, LANES), F32)
     for p in range(6):
         last = jnp.where(lane == p, pltpu.roll(far[p], 64 + p, 1), last)
-    out_ref[0, pl.ds(9, 16, stride=RES), :] = last
+    out_ref[pl.ds(9, 32, stride=RES), :] = last
     for q in range(3):
         pair = jnp.where(lane < 64, far[2 * q], pltpu.roll(far[2 * q + 1], 64, 1))
-        out_ref[0, pl.ds(6 + q, 16, stride=RES), :] = pair
-    out_ref[1] = out_ref[0]
+        out_ref[pl.ds(6 + q, 32, stride=RES), :] = pair
 
 
 def total_kernel(pieces_ref, out_ref):
@@ -284,23 +278,23 @@
         out_specs=vmem(2),
         out_shape=[
             jax.ShapeDtypeStruct((216, LANES), F32),
-            jax.ShapeDtypeStruct((4, 16 * MSG, LANES), F32),
+            jax.ShapeDtypeStruct((2, 32 * MSG, LANES), F32),
         ],
         compiler_params=SMALL,
         name="trace",
     )(keep, got)
-    gathered = exchange(messages, ("z", "y", "x"), MSG)
+    gathered = exchange(messages, ("zh", "zl", "y", "x"), MSG).reshape(4, 16 * MSG, LANES)
     partial, planes = pl.pallas_call(
         correlate_kernel,
         in_specs=vmem(2),
         out_specs=vmem(1) + [pl.BlockSpec(memory_space=pltpu.HBM)],
         out_shape=[
-            jax.ShapeDtypeStruct((2, 16 * RES, LANES), F32),
+            jax.ShapeDtypeStruct((32 * RES, LANES), F32),
             jax.ShapeDtypeStruct((216, LANES), F32),
         ],
         scratch_shapes=[
-            pltpu.VMEM((3, 288, LANES), F32),
-            pltpu.VMEM((2, 96, LANES), F32),
+            pltpu.VMEM((2, 384, LANES), F32),
+            pltpu.VMEM((2, 192, LANES), F32),
             pltpu.SemaphoreType.DMA,
         ],
         compiler_params=SMALL,
@@ -310,7 +304,8 @@
         planes.reshape(6, 18, 2, LANES).transpose(0, 2, 1, 3),
         Layout((0, 2, 1, 3)),
     ).reshape(6, 2, 2304)
-    pieces = exchange(partial, ("ta", "y", "x"), RES)
+    partial = partial + lax.ppermute(partial, "ta", [(0, 1), (1, 0)])
+    pieces = exchange(partial, ("zl", "y", "x"), RES)
     correlator = pl.pallas_call(
         total_kernel,
         in_specs=vmem(1),
@@ -318,19 +313,20 @@
         out_shape=jax.ShapeDtypeStruct((6, 193), F32),
         compiler_params=SMALL,
         name="total",
-    )(pieces.reshape(32 * RES, LANES))
+    )(pieces)
     return loop_planes, correlator
 
 
 def exchange(values, axes, rows):
     shape = values.shape
-    values = values.reshape(-1, rows // 2, 2, LANES)
+    tile = 2 - rows % 2
+    values = values.reshape(-1, rows // tile, tile, LANES)
     return lax.all_to_all(values, axes, split_axis=0, concat_axis=0, tiled=True).reshape(shape)
 
 
 def solution(mesh):
-    grid = Mesh(mesh.devices.reshape(2, 4, 4, 4), ("ta", "z", "y", "x"))
-    gx = ("z", "y", "x")
+    grid = Mesh(mesh.devices.reshape(2, 2, 2, 4, 4), ("ta", "zh", "zl", "y", "x"))
+    gx = ("zh", "zl", "y", "x")
     return jax.shard_map(
         per_device,
         mesh=grid,

time: 43.2 us -> 42.2 us (0.977)
  blocking collectives: 35.4 us -> 31.3 us
  starting transfers between devices: 1.46 us -> 3.15 us
  waiting for transfers between devices: 0.07 us -> 1.1 us
    all_to_all x2, blocking collectives: 35.4 us -> 31.3 us  [exchange(): lax.all_to_all(values, axes, split_axis=0, concat_axis=0, tiled=True)]
    ppermute x0 -> x1, starting transfers between devices: none -> 1.69 us  [per_device(): partial = partial + lax.ppermute(partial, 'ta', [(0, 1), (1, 0)])]
    ppermute x0 -> x1, waiting for transfers between devices: none -> 1.03 us  [per_device(): partial = partial + lax.ppermute(partial, 'ta', [(0, 1), (1, 0)])]
  transfers between devices with their start and end apart: 1 -> 2, of which waited for: 1 -> 2; matrix products, arithmetic and copies ran while one was open for 0% -> 0% of each run, Pallas kernels for 4% -> 4%
where the time goes in v5:
time: 42.2 us; the launch traced here: 41.6 us
  blocking collectives  31.3 us (74%)
  Pallas kernels  5.43 us (13%)
  starting transfers between devices  3.15 us (7%)
  waiting for transfers between devices  1.1 us (3%)
  between operations  0.66 us (2%)
    all_to_all x2, blocking collectives, exchange(): lax.all_to_all(values, axes, split_axis=0, concat_axis=0, tiled=True)  31.3 us
    pallas_call x1, Pallas kernels, product(): pl.pallas_call(sent_kernel, in_specs=hbm, out_specs=vmem(2), out_shape=[j...  1.94 us
    pallas_call x1, Pallas kernels, product(): pl.pallas_call(kept_kernel, in_specs=hbm + vmem(1), out_specs=pl.BlockSpe...  1.69 us
    ppermute x1, starting transfers between devices, per_device(): partial = partial + lax.ppermute(partial, 'ta', [(0, 1), (1, 0)])  1.69 us
    ppermute x1, starting transfers between devices, product(): got = lax.ppermute(sent, 'ta', [(0, 1), (1, 0)])  1.46 us
    ppermute x1, waiting for transfers between devices, per_device(): partial = partial + lax.ppermute(partial, 'ta', [(0, 1), (1, 0)])  1.03 us
    pallas_call x1, Pallas kernels, per_device(): pl.pallas_call(correlate_kernel, in_specs=vmem(2), out_specs=vmem(1) + [p...  0.87 us
  transfers between devices with their start and end apart: 2, of which 2 were waited for; matrix products, arithmetic and copies ran while one was open for 0% of the time, Pallas kernels for 4%

profile of v5, /device:TPU:1, one launch (start us, length us, event | category | flops | bytes accessed | tf_op | source)
XLA Modules:
  0.0 41.6 jit_solution(18222576479826197795)
XLA Ops:
  0.6 1.9 %product_sent.1 = (f32[12,108,128]{2,1,0:T(8,128)S(1)}, f32[2,3,2,3,40,128]{5,4,3,2,1,0:T(8,128)S(1)}) custom-call(f32[3,3,3,432,128]{4,3,2,1,0:T(8,128)} %bitcast.17), custom_call_target="tpu_custom_call" | custom-call | flops 40000000 | bytes 2000000 | tf_op jit(solution)/shard_map/product_sent/pallas_call | solution.py:117
  2.6 1.5 %collective-permute-start = (f32[12,108,128]{2,1,0:T(8,128)S(1)}, f32[12,108,128]{2,1,0:T(8,128)S(1)}, u32[]{:S(2)}, u32[]{:S(2)}) collective-permute-start(f32[12,108,128]{2,1,0:T(8,128)S(1)} %get-tuple-element.9), channel_id=1, source_target_pairs={{0,64},{64,0},{1,65},{65,1},{2,66},{66,2},{3,67},{67,3},{4,68},{68... | collective-permute-start | bytes 1990664 | tf_op jit(solution)/shard_map/ppermute | solution.py:134
  4.0 1.7 %product_kept.1.keep_ref = f32[18,108,128]{2,1,0:T(8,128)S(1)} custom-call(f32[3,3,3,432,128]{4,3,2,1,0:T(8,128)} %bitcast.18, f32[2,3,2,3,40,128]{5,4,3,2,1,0:T(8,128)S(1)} %get-tuple-element.8.early), custom_call_target="tpu_custom_call" | custom-call | flops 40000000 | bytes 2000000 | tf_op jit(solution)/shard_map/product_kept/pallas_call | solution.py:135
  5.7 0.1 collective-permute-done.got_ref
  5.8 0.3 trace.1
  6.1 20.6 %all_to_all.10 = f32[64,7,1,128]{3,2,1,0:T(1,128)S(1)} all-to-all(f32[64,7,1,128]{3,2,1,0:T(1,128)S(1)} %bitcast.16), channel_id=1, replica_groups=mesh['ta'=2,'zh'=2,'zl'=2,'y'=4,'x'=4] {'zh','zl','y','x'}, dimensions={0} | all-to-all | bytes 458752 | tf_op jit(solution)/shard_map/all_to_all | solution.py:324
  26.7 0.9 %correlate.1 = (f32[320,128]{1,0:T(8,128)S(1)}, f32[216,128]{1,0:T(8,128)}) custom-call(f32[4,112,128]{2,1,0:T(8,128)S(1)} %bitcast.14, f32[216,128]{1,0:T(8,128)S(1)} %get-tuple-element.11.planes_ref), custom_call_target="tpu_custom_call" | custom-call | tf_op jit(solution)/shard_map/correlate/pallas_call | solution.py:287
  27.6 1.7 %collective-permute-start.1 = (f32[320,128]{1,0:T(8,128)S(1)}, f32[320,128]{1,0:T(8,128)S(1)}, u32[]{:S(2)}, u32[]{:S(2)}) collective-permute-start(f32[320,128]{1,0:T(8,128)S(1)} %get-tuple-element.13), channel_id=1, source_target_pairs={{0,64},{64,0},{1,65},{65,1},{2,66},{66,2},{3,67},{67,3},{4,68},{68... | collective-permute-start | bytes 491528 | tf_op jit(solution)/shard_map/ppermute | solution.py:307
  29.3 1.0 %collective-permute-done.1 = f32[320,128]{1,0:T(8,128)S(1)} collective-permute-done((f32[320,128]{1,0:T(8,128)S(1)}, f32[320,128]{1,0:T(8,128)S(1)}, u32[]{:S(2)}, u32[]{:S(2)}) %collective-permute-start.1) | collective-permute-done | bytes 163872 | tf_op jit(solution)/shard_map/ppermute | solution.py:307
  30.3 10.6 %all_to_all.11 = f32[32,5,2,128]{3,2,1,0:T(2,128)S(1)} all-to-all(f32[32,5,2,128]{3,2,1,0:T(2,128)S(1)} %bitcast.19), channel_id=1, replica_groups=mesh['ta'=2,'zh'=2,'zl'=2,'y'=4,'x'=4] {'zl','y','x'}, dimensions={0} | all-to-all | bytes 327680 | tf_op jit(solution)/shard_map/all_to_all | solution.py:324
  41.0 0.7 %total.1 = f32[6,193]{1,0:T(8,128)} custom-call(f32[320,128]{1,0:T(8,128)S(1)} %bitcast.15), custom_call_target="tpu_custom_call" | custom-call | tf_op jit(solution)/shard_map/total/pallas_call | solution.py:309
  (1 shorter events, 0.0 us)
Async XLA Ops:
  2.6 3.2 %collective-permute-start = (f32[12,108,128]{2,1,0:T(8,128)S(1)}, f32[12,108,128]{2,1,0:T(8,128)S(1)}, u32[]{:S(2)}, u32[]{:S(2)}) collective-permute-start(f32[12,108,128]{2,1,0:T(8,128)S(1)} %get-tuple-element.9), channel_id=1, source_target_pairs={{0,64},{64,0},{1,65},{65,1},{2,66},{66,2},{3,67},{67,3},{4,68},{68... | collective-permute-start | bytes 1990664 | tf_op jit(solution)/shard_map/ppermute | solution.py:134
  27.6 2.7 %collective-permute-start.1 = (f32[320,128]{1,0:T(8,128)S(1)}, f32[320,128]{1,0:T(8,128)S(1)}, u32[]{:S(2)}, u32[]{:S(2)}) collective-permute-start(f32[320,128]{1,0:T(8,128)S(1)} %get-tuple-element.13), channel_id=1, source_target_pairs={{0,64},{64,0},{1,65},{65,1},{2,66},{66,2},{3,67},{67,3},{4,68},{68... | collective-permute-start | bytes 491528 | tf_op jit(solution)/shard_map/ppermute | solution.py:307

commit v6 on v5

--- a/solution.py
+++ b/solution.py
@@ -80,7 +80,11 @@
         for i, row in enumerate(rows):
             for j in range(3):
                 for c in range(2):
-                    out_ref[6 * i + 2 * j + c, pl.ds(18 * x + start, count), :] = row[j][c]
+                    m = 6 * i + 2 * j + c
+                    if len(out_ref.shape) == 2:
+                        out_ref[pl.ds(108 * m + 18 * x + start, count), :] = row[j][c]
+                    else:
+                        out_ref[m, pl.ds(18 * x + start, count), :] = row[j][c]
 
 
 EARLY = 2
@@ -119,7 +123,7 @@
         in_specs=hbm,
         out_specs=vmem(2),
         out_shape=[
-            jax.ShapeDtypeStruct((12, 108, LANES), F32),
+            jax.ShapeDtypeStruct((1296, LANES), F32),
             jax.ShapeDtypeStruct((EARLY, 3, 2, 3, 40, LANES), F32),
         ],
         scratch_shapes=[
@@ -152,10 +156,15 @@
     for start in range(0, 108, 8):
         count = min(8, 108 - start)
 
+        def at(ref, m):
+            if len(ref.shape) == 2:
+                return ref[pl.ds(108 * m + start, count), :]
+            return ref[m, pl.ds(start, count), :]
+
         def load(ref, rows):
             return [
                 [
-                    tuple(ref[6 * i + 2 * j + c, pl.ds(start, count), :] for c in range(2))
+                    tuple(at(ref, 6 * i + 2 * j + c) for c in range(2))
                     for j in range(3)
                 ]
                 for i in range(rows)

time: 42.2 us -> 42.2 us (level)
  transfers between devices with their start and end apart: 2 -> 2, of which waited for: 2 -> 1; matrix products, arithmetic and copies ran while one was open for 0% -> 0% of each run, Pallas kernels for 4% -> 4%
where the time goes in v6:
time: 42.2 us; the launch traced here: 41.6 us
  blocking collectives  31.3 us (74%)
  Pallas kernels  5.43 us (13%)
  starting transfers between devices  3.15 us (7%)
  waiting for transfers between devices  1.07 us (3%)
  between operations  0.66 us (2%)
    all_to_all x2, blocking collectives, exchange(): lax.all_to_all(values, axes, split_axis=0, concat_axis=0, tiled=True)  31.3 us
    pallas_call x1, Pallas kernels, product(): pl.pallas_call(sent_kernel, in_specs=hbm, out_specs=vmem(2), out_shape=[j...  1.94 us
    pallas_call x1, Pallas kernels, product(): pl.pallas_call(kept_kernel, in_specs=hbm + vmem(1), out_specs=pl.BlockSpe...  1.69 us
    ppermute x1, starting transfers between devices, per_device(): partial = partial + lax.ppermute(partial, 'ta', [(0, 1), (1, 0)])  1.69 us
    ppermute x1, starting transfers between devices, product(): got = lax.ppermute(sent, 'ta', [(0, 1), (1, 0)])  1.46 us
    ppermute x1, waiting for transfers between devices, per_device(): partial = partial + lax.ppermute(partial, 'ta', [(0, 1), (1, 0)])  1.03 us
    pallas_call x1, Pallas kernels, per_device(): pl.pallas_call(correlate_kernel, in_specs=vmem(2), out_specs=vmem(1) + [p...  0.87 us
  transfers between devices with their start and end apart: 2, of which 1 were waited for; matrix products, arithmetic and copies ran while one was open for 0% of the time, Pallas kernels for 4%

profile of v6, /device:TPU:1, one launch (start us, length us, event | category | flops | bytes accessed | tf_op | source)
XLA Modules:
  0.0 41.6 jit_solution(3548570912298848098)
XLA Ops:
  0.6 1.9 %product_sent.1 = (f32[1296,128]{1,0:T(8,128)S(1)}, f32[2,3,2,3,40,128]{5,4,3,2,1,0:T(8,128)S(1)}) custom-call(f32[3,3,3,432,128]{4,3,2,1,0:T(8,128)} %bitcast.17), custom_call_target="tpu_custom_call" | custom-call | flops 40000000 | bytes 2000000 | tf_op jit(solution)/shard_map/product_sent/pallas_call | solution.py:121
  2.6 1.5 %collective-permute-start = (f32[1296,128]{1,0:T(8,128)S(1)}, f32[1296,128]{1,0:T(8,128)S(1)}, u32[]{:S(2)}, u32[]{:S(2)}) collective-permute-start(f32[1296,128]{1,0:T(8,128)S(1)} %get-tuple-element.9), channel_id=1, source_target_pairs={{0,64},{64,0},{1,65},{65,1},{2,66},{66,2},{3,67},{67,3},{4,68},{68... | collective-permute-start | bytes 1990664 | tf_op jit(solution)/shard_map/ppermute | solution.py:138
  4.0 1.7 %product_kept.1.keep_ref = f32[18,108,128]{2,1,0:T(8,128)S(1)} custom-call(f32[3,3,3,432,128]{4,3,2,1,0:T(8,128)} %bitcast.18, f32[2,3,2,3,40,128]{5,4,3,2,1,0:T(8,128)S(1)} %get-tuple-element.8.early), custom_call_target="tpu_custom_call" | custom-call | flops 40000000 | bytes 2000000 | tf_op jit(solution)/shard_map/product_kept/pallas_call | solution.py:139
  5.7 0.0 collective-permute-done.got_ref
  5.8 0.3 trace.1
  6.0 20.6 %all_to_all.10 = f32[64,7,1,128]{3,2,1,0:T(1,128)S(1)} all-to-all(f32[64,7,1,128]{3,2,1,0:T(1,128)S(1)} %bitcast.16), channel_id=1, replica_groups=mesh['ta'=2,'zh'=2,'zl'=2,'y'=4,'x'=4] {'zh','zl','y','x'}, dimensions={0} | all-to-all | bytes 458752 | tf_op jit(solution)/shard_map/all_to_all | solution.py:333
  26.7 0.9 %correlate.1 = (f32[320,128]{1,0:T(8,128)S(1)}, f32[216,128]{1,0:T(8,128)}) custom-call(f32[4,112,128]{2,1,0:T(8,128)S(1)} %bitcast.14, f32[216,128]{1,0:T(8,128)S(1)} %get-tuple-element.11.planes_ref), custom_call_target="tpu_custom_call" | custom-call | tf_op jit(solution)/shard_map/correlate/pallas_call | solution.py:296
  27.5 1.7 %collective-permute-start.1 = (f32[320,128]{1,0:T(8,128)S(1)}, f32[320,128]{1,0:T(8,128)S(1)}, u32[]{:S(2)}, u32[]{:S(2)}) collective-permute-start(f32[320,128]{1,0:T(8,128)S(1)} %get-tuple-element.13), channel_id=1, source_target_pairs={{0,64},{64,0},{1,65},{65,1},{2,66},{66,2},{3,67},{67,3},{4,68},{68... | collective-permute-start | bytes 491528 | tf_op jit(solution)/shard_map/ppermute | solution.py:316
  29.2 1.0 %collective-permute-done.1 = f32[320,128]{1,0:T(8,128)S(1)} collective-permute-done((f32[320,128]{1,0:T(8,128)S(1)}, f32[320,128]{1,0:T(8,128)S(1)}, u32[]{:S(2)}, u32[]{:S(2)}) %collective-permute-start.1) | collective-permute-done | bytes 163872 | tf_op jit(solution)/shard_map/ppermute | solution.py:316
  30.3 10.6 %all_to_all.11 = f32[32,5,2,128]{3,2,1,0:T(2,128)S(1)} all-to-all(f32[32,5,2,128]{3,2,1,0:T(2,128)S(1)} %bitcast.19), channel_id=1, replica_groups=mesh['ta'=2,'zh'=2,'zl'=2,'y'=4,'x'=4] {'zl','y','x'}, dimensions={0} | all-to-all | bytes 327680 | tf_op jit(solution)/shard_map/all_to_all | solution.py:333
  40.9 0.7 %total.1 = f32[6,193]{1,0:T(8,128)} custom-call(f32[320,128]{1,0:T(8,128)S(1)} %bitcast.15), custom_call_target="tpu_custom_call" | custom-call | tf_op jit(solution)/shard_map/total/pallas_call | solution.py:318
  (1 shorter events, 0.0 us)
Async XLA Ops:
  2.6 3.2 %collective-permute-start = (f32[1296,128]{1,0:T(8,128)S(1)}, f32[1296,128]{1,0:T(8,128)S(1)}, u32[]{:S(2)}, u32[]{:S(2)}) collective-permute-start(f32[1296,128]{1,0:T(8,128)S(1)} %get-tuple-element.9), channel_id=1, source_target_pairs={{0,64},{64,0},{1,65},{65,1},{2,66},{66,2},{3,67},{67,3},{4,68},{68... | collective-permute-start | bytes 1990664 | tf_op jit(solution)/shard_map/ppermute | solution.py:138
  27.5 2.7 %collective-permute-start.1 = (f32[320,128]{1,0:T(8,128)S(1)}, f32[320,128]{1,0:T(8,128)S(1)}, u32[]{:S(2)}, u32[]{:S(2)}) collective-permute-start(f32[320,128]{1,0:T(8,128)S(1)} %get-tuple-element.13), channel_id=1, source_target_pairs={{0,64},{64,0},{1,65},{65,1},{2,66},{66,2},{3,67},{67,3},{4,68},{68... | collective-permute-start | bytes 491528 | tf_op jit(solution)/shard_map/ppermute | solution.py:316
